TPU v7x, 32 devices: a whole 2x2x4 slice. The times are simulated.
32 devices in a mesh: dp: 8 (over z, core), expert: 4 (over y, x).
Axes of the slice: x: 2, y: 2, z: 4, core: 2. Of those that a mesh axis runs over, the one named last changes fastest.
Arguments:
- tokens: bfloat16 [16384, 2048], P(('dp', 'expert')), parts along dimension 0, may hold values from -6 to 6
- modality: int32 [16384], P(('dp', 'expert')), parts along dimension 0, may hold values 0 or 1
- expert_ids: int32 [16384, 2], P(('dp', 'expert')), parts along dimension 0, may hold values from 0 to 3, all different within a row; in each aligned block of 512 rows (0 to 511, 512 to 1023, ...) at most 320 rows name the same one
- route_weights: float32 [16384, 2], P(('dp', 'expert')), parts along dimension 0, may hold values from 0.25 to 1
- norm_gain: float32 [2, 2048], replicated, may hold values from 0.25 to 1.75
- gate_weight: bfloat16 [2048, 3584], P(None, 'expert'), may hold values from -0.125 to 0.125
- up_weight: bfloat16 [2048, 3584], P(None, 'expert'), may hold values from -0.125 to 0.125
- down_weight: bfloat16 [3584, 2048], P('expert'), may hold values from -0.1875 to 0.1875
Outputs:
- mixed: bfloat16 [16384, 2048], P(('dp', 'expert')), parts along dimension 0
There are 8 independent parts, one for each index of `dp`. A program takes and returns all parts, laid end to end along the dimension named above; an argument that names none is the same for every part. Nothing has to cross between parts.
Inputs may be any that keep to these rules, and one draw needn't show every extreme that they name: `expert_ids`: each row names 2 different experts. Among the rows of one device no expert is named by more than 320 rows, a bound that some blocks reach.
All inputs are finite; a program needn't handle non-finite values. No bound on the sum of `modality` on one device may be relied on, other than what follows from the above.
Results may differ from a plain program's by a relative error of at most 0.0054.
Values may be sent and summed in bfloat16 or wider, within the bound.
A program may use at most 128 MiB of HBM per device.

v0:
```python
import functools

import jax
import jax.numpy as jnp
from jax import lax
from jax.experimental import pallas as pl
from jax.experimental.pallas import tpu as pltpu
from jax.sharding import PartitionSpec as P

epsilon = 1e-05
LANES = 128
AXIS = "expert"


def grid_side(devices):
    side = 1
    while side * side < devices:
        side += 1
    return side if side * side == devices else devices


def moe_kernel(
    devices,
    tokens_hbm,
    modality_ref,
    ids_ref,
    weights_ref,
    gain_ref,
    gate_hbm,
    up_hbm,
    down_hbm,
    out_ref,
    tokens,
    gate,
    up,
    down,
    normed,
    total,
    place_rows,
    place_cols,
    share_cols,
    packed,
    arrived,
    finished,
    returned,
    load_sem,
    go_send,
    go_recv,
    back_send,
    back_recv,
):
    waves, _, chunk, width = packed.shape
    tok_rows = tokens.shape[0]
    fanout = ids_ref.shape[0]
    me = lax.axis_index(AXIS)
    side = grid_side(devices)
    mine_hi, mine_lo = me // side, me % side
    lines = devices // side

    def ahead(step):
        return ((mine_hi + step // side) % lines) * side + (mine_lo + step % side) % side

    def behind(step):
        return ((mine_hi + lines - step // side) % lines) * side + (
            mine_lo + side - step % side
        ) % side

    def go(wave, step):
        return pltpu.make_async_remote_copy(
            src_ref=packed.at[wave, step],
            dst_ref=arrived.at[wave, step],
            send_sem=go_send.at[wave, step],
            recv_sem=go_recv.at[wave, step],
            device_id={AXIS: ahead(step)},
            device_id_type=pl.DeviceIdType.MESH,
        )

    def back(wave, step):
        return pltpu.make_async_remote_copy(
            src_ref=finished.at[wave, step],
            dst_ref=returned.at[wave, step],
            send_sem=back_send.at[wave, step],
            recv_sem=back_recv.at[wave, step],
            device_id={AXIS: behind(step)},
            device_id_type=pl.DeviceIdType.MESH,
        )

    loads = [
        pltpu.make_async_copy(tokens_hbm, tokens, load_sem.at[0]),
        pltpu.make_async_copy(gate_hbm, gate, load_sem.at[1]),
        pltpu.make_async_copy(up_hbm, up, load_sem.at[2]),
        pltpu.make_async_copy(down_hbm, down, load_sem.at[3]),
    ]
    for load in loads:
        load.start()

    barrier = pltpu.get_barrier_semaphore()

    def greet(step, carry):
        pl.semaphore_signal(
            barrier, inc=1, device_id={AXIS: ahead(step)}, device_id_type=pl.DeviceIdType.MESH
        )
        return carry

    lax.fori_loop(1, devices, greet, 0)

    expert = lax.broadcasted_iota(jnp.int32, (LANES, tok_rows), 0)
    named = jnp.zeros((LANES, tok_rows), jnp.float32)
    share = jnp.zeros((LANES, tok_rows), jnp.float32)
    for k in range(fanout):
        hit = expert == ids_ref[k : k + 1, :]
        named = jnp.where(hit, 1.0, named)
        share = jnp.where(hit, weights_ref[k : k + 1, :], share)
    before = (
        lax.broadcasted_iota(jnp.int32, (tok_rows, tok_rows), 0)
        < lax.broadcasted_iota(jnp.int32, (tok_rows, tok_rows), 1)
    )
    count = jnp.dot(
        named.astype(jnp.bfloat16),
        jnp.where(before, 1.0, 0.0).astype(jnp.bfloat16),
        preferred_element_type=jnp.float32,
    )
    place = jnp.where(named > 0.5, count, -1.0)
    place_rows[...] = place
    place_cols[...] = place.T
    share_cols[...] = share.T
    image = jnp.broadcast_to(modality_ref[...].astype(jnp.float32), (LANES, tok_rows)).T

    loads[0].wait()
    rows = 64
    for start in range(0, tok_rows, rows):
        values = tokens[start : start + rows, :].astype(jnp.float32)
        square = jnp.mean(values * values, axis=1, keepdims=True)
        gains = jnp.where(
            image[start : start + rows, :1] > 0.5, gain_ref[1:2, :], gain_ref[0:1, :]
        )
        normed[start : start + rows, :] = (
            values * lax.rsqrt(square + epsilon) * gains
        ).astype(jnp.bfloat16)

    def pack(wave, step, target):
        line = place_rows[pl.ds(ahead(step), 1), :]
        slot = lax.broadcasted_iota(jnp.int32, (chunk, tok_rows), 0) + wave * chunk
        pick = jnp.where(line == slot.astype(jnp.float32), 1.0, 0.0).astype(jnp.bfloat16)
        target[wave, step] = jnp.dot(
            pick, normed[...], preferred_element_type=jnp.float32
        ).astype(jnp.bfloat16)

    others = devices - 1
    items = waves * others

    def which(item):
        return item // others, others - item % others

    pl.semaphore_wait(barrier, others)

    def send(item, carry):
        wave, step = which(item)
        pack(wave, step, packed)
        go(wave, step).start()
        return carry

    lax.fori_loop(0, items, send, 0)

    for load in loads[1:]:
        load.wait()

    def feed(source, target, wave, step):
        value = source[wave, step]
        opened = jnp.dot(value, gate[...], preferred_element_type=jnp.float32)
        upper = jnp.dot(value, up[...], preferred_element_type=jnp.float32)
        active = (opened / (1.0 + jnp.exp(-opened)) * upper).astype(jnp.bfloat16)
        target[wave, step] = jnp.dot(
            active, down[...], preferred_element_type=jnp.float32
        ).astype(jnp.bfloat16)

    def spread(wave, step):
        lane = lax.broadcasted_iota(jnp.int32, (tok_rows, LANES), 1) == ahead(step)
        line = jnp.sum(jnp.where(lane, place_cols[...], 0.0), axis=1, keepdims=True)
        worth = jnp.sum(jnp.where(lane, share_cols[...], 0.0), axis=1, keepdims=True)
        slot = lax.broadcasted_iota(jnp.int32, (tok_rows, chunk), 1) + wave * chunk
        spots = jnp.where(line == slot.astype(jnp.float32), worth, 0.0)
        high = spots.astype(jnp.bfloat16)
        low = (spots - high.astype(jnp.float32)).astype(jnp.bfloat16)
        value = returned[wave, step]
        return jnp.dot(high, value, preferred_element_type=jnp.float32) + jnp.dot(
            low, value, preferred_element_type=jnp.float32
        )

    total[...] = tokens[...].astype(jnp.float32)

    def local(wave, carry):
        pack(wave, 0, arrived)
        feed(arrived, returned, wave, 0)
        total[...] += spread(wave, 0)
        return carry

    lax.fori_loop(0, waves, local, 0)

    def serve(item, carry):
        wave, step = which(item)
        go(wave, step).wait_recv()
        feed(arrived, finished, wave, step)
        back(wave, step).start()
        return carry

    lax.fori_loop(0, items, serve, 0)

    def collect(item, carry):
        wave, step = which(item)
        back(wave, step).wait_recv()
        total[...] += spread(wave, step)
        return carry

    lax.fori_loop(0, items - 1, collect, 0)
    wave, step = which(items - 1)
    back(wave, step).wait_recv()
    out_ref[...] = (total[...] + spread(wave, step)).astype(out_ref.dtype)

    def settle(item, carry):
        wave, step = which(item)
        go(wave, step).wait_send()
        back(wave, step).wait_send()
        return carry

    lax.fori_loop(0, items, settle, 0)


def relay_kernel(
    blocks,
    tokens_hbm,
    modality_hbm,
    ids_hbm,
    weights_hbm,
    gain_hbm,
    gate_hbm,
    up_hbm,
    down_hbm,
    out_ref,
    modality_ref,
    ids_ref,
    weights_ref,
    gain_ref,
    tokens,
    near_tokens,
    gate,
    up,
    down,
    normed,
    near_normed,
    total,
    near_total,
    facts,
    near_facts,
    packed,
    arrived,
    finished,
    returned,
    own_rows,
    own_results,
    sum_out,
    sum_in,
    load_sem,
    token_sem,
    facts_sem,
    dense_send,
    dense_recv,
    go_send,
    go_recv,
    back_send,
    back_recv,
    sum_send,
    sum_recv,
):
    _, capacity, width = packed.shape
    waves = go_send.shape[1]
    chunk = capacity // waves
    tok_rows = tokens.shape[0]
    part = tok_rows // blocks
    fanout = ids_ref.shape[0]
    me = lax.axis_index(AXIS)
    role = lax.axis_index("dp") % 2
    high, low = me // 2, me % 2
    beside = high * 2 + 1 - low
    above = (1 - high) * 2 + low
    first = beside * (1 - role) + above * role
    second = above * (1 - role) + beside * role

    def remote(source, target, send_sem, recv_sem, peer):
        return pltpu.make_async_remote_copy(
            src_ref=source,
            dst_ref=target,
            send_sem=send_sem,
            recv_sem=recv_sem,
            device_id={AXIS: peer},
            device_id_type=pl.DeviceIdType.MESH,
        )

    def part_rows(block):
        return pl.ds(pl.multiple_of(block * part, part), part)

    def wave_rows(wave):
        return pl.ds(pl.multiple_of(wave * chunk, chunk), chunk)

    def dense(block):
        rows = part_rows(block)
        return remote(
            tokens.at[rows], near_tokens.at[rows], dense_send.at[block], dense_recv.at[block], first
        )

    def go(kind, wave):
        rows = wave_rows(wave)
        return remote(
            packed.at[kind, rows],
            arrived.at[kind, rows],
            go_send.at[kind, wave],
            go_recv.at[kind, wave],
            second,
        )

    def back(kind, wave):
        rows = wave_rows(wave)
        return remote(
            finished.at[kind, rows],
            returned.at[kind, rows],
            back_send.at[kind, wave],
            back_recv.at[kind, wave],
            second,
        )

    def sums(block):
        rows = part_rows(block)
        return remote(
            sum_out.at[rows], sum_in.at[rows], sum_send.at[block], sum_recv.at[block], first
        )

    def each(count, step):
        def body(index, carry):
            step(index)
            return carry

        lax.fori_loop(0, count, body, 0)

    loads = [
        pltpu.make_async_copy(source, target, load_sem.at[index])
        for index, (source, target) in enumerate(
            (
                (ids_hbm, ids_ref),
                (weights_hbm, weights_ref),
                (modality_hbm, modality_ref),
                (gain_hbm, gain_ref),
                (gate_hbm, gate),
                (up_hbm, up),
                (down_hbm, down),
            )
        )
    ]

    def token_load(block):
        rows = part_rows(block)
        return pltpu.make_async_copy(tokens_hbm.at[rows], tokens.at[rows], token_sem.at[block])

    each(blocks, lambda block: token_load(block).start())
    for load in loads[:4]:
        load.start()
    barrier = pltpu.get_barrier_semaphore()
    for peer in (first, second):
        pl.semaphore_signal(
            barrier, inc=1, device_id={AXIS: peer}, device_id_type=pl.DeviceIdType.MESH
        )
    pl.semaphore_wait(barrier, 2)

    def leave(block):
        token_load(block).wait()
        dense(block).start()

    each(blocks, leave)
    for load in loads[4:]:
        load.start()
    for load in loads[:4]:
        load.wait()

    lines = 8
    expert = lax.broadcasted_iota(jnp.int32, (lines, tok_rows), 0)
    named = jnp.zeros((lines, tok_rows), jnp.float32)
    share = jnp.zeros((lines, tok_rows), jnp.float32)
    for k in range(fanout):
        hit = expert == ids_ref[k : k + 1, :]
        named = jnp.where(hit, 1.0, named)
        share = jnp.where(hit, weights_ref[k : k + 1, :], share)
    before = (
        lax.broadcasted_iota(jnp.int32, (tok_rows, tok_rows), 0)
        < lax.broadcasted_iota(jnp.int32, (tok_rows, tok_rows), 1)
    )
    count = jnp.dot(
        named.astype(jnp.bfloat16),
        jnp.where(before, 1.0, 0.0).astype(jnp.bfloat16),
        preferred_element_type=jnp.float32,
    )
    facts[0:lines, :] = jnp.where(named > 0.5, count, -1.0)
    facts[lines : 2 * lines, :] = share
    facts[2 * lines : 3 * lines, :] = jnp.broadcast_to(
        modality_ref[...].astype(jnp.float32), (lines, tok_rows)
    )
    told = remote(facts, near_facts, facts_sem.at[0], facts_sem.at[1], first)
    told.start()

    def column(line):
        return jnp.broadcast_to(line, (LANES, tok_rows)).T[:, :1]

    def normalize_rows(source, target, image, start, rows):
        values = source[start : start + rows, :].astype(jnp.float32)
        square = jnp.mean(values * values, axis=1, keepdims=True)
        gains = jnp.where(
            image[start : start + rows] > 0.5, gain_ref[1:2, :], gain_ref[0:1, :]
        )
        target[start : start + rows, :] = (
            values * lax.rsqrt(square + epsilon) * gains
        ).astype(jnp.bfloat16)

    def pack(notes, rows, who, wave):
        line = notes[pl.ds(who, 1), :]
        slot = lax.broadcasted_iota(jnp.int32, (chunk, tok_rows), 0) + wave * chunk
        pick = jnp.where(line == slot.astype(jnp.float32), 1.0, 0.0).astype(jnp.bfloat16)
        return jnp.dot(pick, rows[...], preferred_element_type=jnp.float32).astype(jnp.bfloat16)

    def feed(value):
        opened = jnp.dot(value, gate[...], preferred_element_type=jnp.float32)
        upper = jnp.dot(value, up[...], preferred_element_type=jnp.float32)
        active = (opened / (1.0 + jnp.exp(-opened)) * upper).astype(jnp.bfloat16)
        return jnp.dot(active, down[...], preferred_element_type=jnp.float32).astype(jnp.bfloat16)

    def spots(notes, who):
        line = column(notes[pl.ds(who, 1), :])
        worth = column(notes[pl.ds(who + lines, 1), :])
        slot = lax.broadcasted_iota(jnp.int32, (tok_rows, capacity), 1)
        full = jnp.where(line == slot.astype(jnp.float32), worth, 0.0)
        coarse = full.astype(jnp.bfloat16)
        return coarse, (full - coarse.astype(jnp.float32)).astype(jnp.bfloat16)

    def spread(coarse, fine, value):
        return jnp.dot(coarse, value, preferred_element_type=jnp.float32) + jnp.dot(
            fine, value, preferred_element_type=jnp.float32
        )

    image = column(facts[2 * lines : 2 * lines + 1, :])
    rows = 64
    for start in range(0, tok_rows, rows):
        normalize_rows(tokens, normed, image, start, rows)

    def send(wave):
        packed[0, wave_rows(wave)] = pack(facts, normed, second, wave)
        go(0, wave).start()

    each(waves, send)

    for load in loads[4:]:
        load.wait()

    def local(wave):
        here = wave_rows(wave)
        own_results[here] = feed(pack(facts, normed, me, wave))

    each(waves, local)
    total[...] = tokens[...].astype(jnp.float32) + spread(*spots(facts, me), own_results[...])

    def serve(kind, now):
        def step(wave):
            here = wave_rows(wave)
            go(kind, wave).wait_recv()
            finished[kind, here] = feed(arrived[kind, here])

            @pl.when(wave < now)
            def _():
                back(kind, wave).start()

        each(waves, step)

    serve(0, waves - 1)

    told.wait_recv()
    near_image = column(near_facts[2 * lines : 2 * lines + 1, :])
    for block in range(blocks):
        dense(block).wait_recv()
        for start in range(block * part, (block + 1) * part, rows):
            normalize_rows(near_tokens, near_normed, near_image, start, rows)

    def forward(wave):
        packed[1, wave_rows(wave)] = pack(near_facts, near_normed, second, wave)
        go(1, wave).start()

    each(waves, forward)

    def near_local(wave):
        here = wave_rows(wave)
        own_rows[here] = feed(pack(near_facts, near_normed, me, wave))

    each(waves, near_local)
    near_total[...] = spread(*spots(near_facts, me), own_rows[...])

    serve(1, waves)
    back(0, waves - 1).start()

    coarse, fine = spots(near_facts, second)
    each(waves, lambda wave: back(1, wave).wait_recv())
    for block in range(blocks):
        here = slice(block * part, (block + 1) * part)
        sum_out[here, :] = (
            near_total[here, :] + spread(coarse[here], fine[here], returned[1])
        ).astype(jnp.bfloat16)
        sums(block).start()

    each(waves, lambda wave: back(0, wave).wait_recv())
    total[...] += spread(*spots(facts, second), returned[0])

    for block in range(blocks):
        here = slice(block * part, (block + 1) * part)
        sums(block).wait_recv()
        out_ref[here, :] = (total[here, :] + sum_in[here, :].astype(jnp.float32)).astype(
            out_ref.dtype
        )

    told.wait_send()
    each(blocks, lambda block: dense(block).wait_send())
    each(blocks, lambda block: sums(block).wait_send())
    for kind in range(2):
        each(waves, lambda wave: go(kind, wave).wait_send())
        each(waves, lambda wave: back(kind, wave).wait_send())


def relay_scratch(tok_rows, width, hidden, fanout, capacity, waves, blocks):
    dense = pltpu.VMEM((tok_rows, width), jnp.bfloat16)
    sums = pltpu.VMEM((tok_rows, width), jnp.float32)
    facts = pltpu.VMEM((24, tok_rows), jnp.float32)
    slots = pltpu.VMEM((2, capacity, width), jnp.bfloat16)
    single = pltpu.VMEM((capacity, width), jnp.bfloat16)
    wide = pltpu.VMEM((width, hidden), jnp.bfloat16)
    by_block = pltpu.SemaphoreType.DMA((blocks,))
    by_wave = pltpu.SemaphoreType.DMA((2, waves))
    return [
        pltpu.VMEM((1, tok_rows), jnp.int32), pltpu.VMEM((fanout, tok_rows), jnp.int32),
        pltpu.VMEM((fanout, tok_rows), jnp.float32), pltpu.VMEM((2, width), jnp.float32),
        dense, dense, wide, wide, pltpu.VMEM((hidden, width), jnp.bfloat16), dense, dense,
        sums, sums, facts, facts, slots, slots, slots, slots, single, single, dense, dense,
        pltpu.SemaphoreType.DMA((7,)), by_block, pltpu.SemaphoreType.DMA((2,)), by_block, by_block,
        by_wave, by_wave, by_wave, by_wave, by_block, by_block,
    ]


def direct_scratch(tok_rows, width, hidden, buffer, sems):
    return [
        pltpu.VMEM((tok_rows, width), jnp.bfloat16),
        pltpu.VMEM((width, hidden), jnp.bfloat16),
        pltpu.VMEM((width, hidden), jnp.bfloat16),
        pltpu.VMEM((hidden, width), jnp.bfloat16),
        pltpu.VMEM((tok_rows, width), jnp.bfloat16),
        pltpu.VMEM((tok_rows, width), jnp.float32),
        pltpu.VMEM((LANES, tok_rows), jnp.float32),
        pltpu.VMEM((tok_rows, LANES), jnp.float32),
        pltpu.VMEM((tok_rows, LANES), jnp.float32),
        buffer,
        buffer,
        buffer,
        buffer,
        pltpu.SemaphoreType.DMA((4,)),
        sems,
        sems,
        sems,
        sems,
    ]


def shards(
    tokens, modality, expert_ids, route_weights, norm_gain, gate_weight, up_weight, down_weight
):
    devices = lax.axis_size(AXIS)
    tok_rows, width = tokens.shape
    fanout = expert_ids.shape[1]
    hidden = gate_weight.shape[1]
    capacity = min(tok_rows, tok_rows * fanout * 5 // (4 * devices))
    waves = 2 if capacity % 32 == 0 and capacity >= 256 else 1
    chunk = capacity // waves
    buffer = pltpu.VMEM((waves, devices, chunk, width), jnp.bfloat16)
    near = pl.BlockSpec(memory_space=pltpu.VMEM)
    far = pl.BlockSpec(memory_space=pl.ANY)
    sems = pltpu.SemaphoreType.DMA((waves, devices))
    blocks = 4
    relayed = devices == 4 and tok_rows % (64 * blocks) == 0 and capacity % 32 == 0
    if relayed:
        kernel = functools.partial(relay_kernel, blocks)
        scratch = relay_scratch(tok_rows, width, hidden, fanout, capacity, 2, blocks)
    else:
        kernel = functools.partial(moe_kernel, devices)
        scratch = direct_scratch(tok_rows, width, hidden, buffer, sems)
    return pl.pallas_call(
        kernel,
        out_shape=pltpu.VMEM((tok_rows, width), jnp.bfloat16),
        in_specs=[far] + [far if relayed else near] * 4 + [far] * 3,
        out_specs=near,
        scratch_shapes=scratch,
        compiler_params=pltpu.CompilerParams(
            collective_id=0, has_side_effects=True, vmem_limit_bytes=58 * 1024 * 1024
        ),
    )(
        tokens,
        modality.reshape(1, tok_rows),
        expert_ids.T,
        route_weights.T,
        norm_gain,
        gate_weight,
        up_weight,
        down_weight,
    )


def solution(mesh):
    placed = (
        P(("dp", AXIS), None),
        P(("dp", AXIS)),
        P(("dp", AXIS), None),
        P(("dp", AXIS), None),
        P(),
        P(None, AXIS),
        P(None, AXIS),
        P(AXIS, None),
    )
    return jax.shard_map(
        shards, mesh=mesh, in_specs=placed, out_specs=P(("dp", AXIS), None), check_vma=False
    )
```

profile of v0, /device:TPU:0, one launch (start us, length us, event | category | flops | bytes accessed | tf_op | source)
XLA Modules:
  0.0 111.4 jit_solution(9786516955363469599)
XLA Ops:
  0.0 110.1 %shard_map.82 = bf16[512,2048]{1,0:T(8,128)(2,1)S(1)} custom-call(bf16[512,2048]{1,0:T(8,128)(2,1)} %tokens_hbm.1, s32[1,512]{1,0:T(1,128)} %bitcast.5, s32[2,512]{1,0:T(2,128)} %bitcast.3, f32[2,512]{1,0:T(2,128)} %bitcast.4, f32[2,2048]{1,0:T(2,128)} %gain_hbm.1, bf16[2048,896]{1,0:T(8,128)(2,1)} %gate_hbm.1, bf16[2048,896]{1,0:T(8,128)(2,1)} %up_hbm.1, ...), custom_call_target="tpu_custom_call" | custom-call | tf_op jit(solution)/shard_map/pallas_call | solution.py:595
  110.1 1.3 %copy.10 = bf16[512,2048]{1,0:T(8,128)(2,1)} copy(bf16[512,2048]{1,0:T(8,128)(2,1)S(1)} %shard_map.82) | data formatting | bytes 4194304
where the time goes:
time: 114 us; the launch traced here: 111 us
  Pallas kernels  110 us (96%)
  local copies, waits for them, and re-layouts  1.32 us (1%)
    pallas_call x1, Pallas kernels, shards(): pl.pallas_call(kernel, out_shape=pltpu.VMEM((tok_rows, width), jnp.bfloat...  110 us

commit v1 on v0

--- a/solution.py
+++ b/solution.py
@@ -226,8 +226,10 @@
     lax.fori_loop(0, items, settle, 0)
 
 
-def relay_kernel(
+def pair_kernel(
     blocks,
+    groups,
+    pieces,
     tokens_hbm,
     modality_hbm,
     ids_hbm,
@@ -242,104 +244,121 @@
     weights_ref,
     gain_ref,
     tokens,
+    sorted_tokens,
     near_tokens,
     gate,
     up,
     down,
+    far_gate,
+    far_up,
+    far_down,
     normed,
     near_normed,
     total,
     near_total,
     facts,
+    sorted_facts,
     near_facts,
-    packed,
-    arrived,
-    finished,
-    returned,
-    own_rows,
-    own_results,
+    slots,
+    columns,
     sum_out,
     sum_in,
     load_sem,
-    token_sem,
     facts_sem,
     dense_send,
     dense_recv,
-    go_send,
-    go_recv,
-    back_send,
-    back_recv,
     sum_send,
     sum_recv,
+    wide_send,
+    wide_recv,
+    tall_send,
+    tall_recv,
 ):
-    _, capacity, width = packed.shape
-    waves = go_send.shape[1]
-    chunk = capacity // waves
-    tok_rows = tokens.shape[0]
+    tok_rows, width = tokens.shape
+    hidden = gate.shape[1]
+    fanout = ids_ref.shape[0]
+    devices = lax.axis_size(AXIS)
+    capacity = tok_rows * fanout * 5 // (4 * devices)
     part = tok_rows // blocks
-    fanout = ids_ref.shape[0]
+    free = (tok_rows - capacity) // part
     me = lax.axis_index(AXIS)
-    role = lax.axis_index("dp") % 2
-    high, low = me // 2, me % 2
-    beside = high * 2 + 1 - low
-    above = (1 - high) * 2 + low
-    first = beside * (1 - role) + above * role
-    second = above * (1 - role) + beside * role
-
-    def remote(source, target, send_sem, recv_sem, peer):
+    copy_of = lax.axis_index("dp")
+    layer, core = copy_of // 2, copy_of % 2
+    beside = me // 2 * 2 + 1 - me % 2
+    above = (1 - me // 2) * 2 + me % 2
+    diagonal = (1 - me // 2) * 2 + 1 - me % 2
+    other_layer = (layer // 2 * 2 + 1 - layer % 2) * 2 + core
+    other_core = layer * 2 + 1 - core
+    quarter = layer % 2 * 2 + core
+    layer_quarter = (1 - layer % 2) * 2 + core
+
+    def remote(source, target, send_sem, recv_sem, copy, peer):
         return pltpu.make_async_remote_copy(
             src_ref=source,
             dst_ref=target,
             send_sem=send_sem,
             recv_sem=recv_sem,
-            device_id={AXIS: peer},
+            device_id={"dp": copy, AXIS: peer},
             device_id_type=pl.DeviceIdType.MESH,
         )
 
     def part_rows(block):
         return pl.ds(pl.multiple_of(block * part, part), part)
-
-    def wave_rows(wave):
-        return pl.ds(pl.multiple_of(wave * chunk, chunk), chunk)
 
     def dense(block):
         rows = part_rows(block)
         return remote(
-            tokens.at[rows], near_tokens.at[rows], dense_send.at[block], dense_recv.at[block], first
-        )
-
-    def go(kind, wave):
-        rows = wave_rows(wave)
-        return remote(
-            packed.at[kind, rows],
-            arrived.at[kind, rows],
-            go_send.at[kind, wave],
-            go_recv.at[kind, wave],
-            second,
-        )
-
-    def back(kind, wave):
-        rows = wave_rows(wave)
-        return remote(
-            finished.at[kind, rows],
-            returned.at[kind, rows],
-            back_send.at[kind, wave],
-            back_recv.at[kind, wave],
-            second,
+            sorted_tokens.at[rows],
+            near_tokens.at[rows],
+            dense_send.at[block],
+            dense_recv.at[block],
+            copy_of,
+            beside,
         )
 
     def sums(block):
         rows = part_rows(block)
         return remote(
-            sum_out.at[rows], sum_in.at[rows], sum_send.at[block], sum_recv.at[block], first
-        )
-
-    def each(count, step):
+            sum_out.at[rows], sum_in.at[rows], sum_send.at[block], sum_recv.at[block], copy_of, beside
+        )
+
+    wide_rows = width // 4 // groups
+    tall_rows = hidden // 4 // pieces
+
+    def weight_copy(stage, kind, index):
+        if kind < 2:
+            near, far = ((gate_hbm, far_gate), (up_hbm, far_up))[kind]
+            count, whole, send, recv = wide_rows, width // 4, wide_send.at[kind], wide_recv.at[kind]
+        else:
+            near, far = down_hbm, far_down
+            count, whole, send, recv = tall_rows, hidden // 4, tall_send, tall_recv
+        which = layer_quarter if stage == 3 else quarter
+        rows = pl.ds(pl.multiple_of(which * whole + index * count, count), count)
+        copy, peer = ((copy_of, above), (other_layer, me), (other_core, me), (other_core, me))[stage]
+        return remote(
+            (near if stage == 0 else far).at[rows],
+            far.at[rows],
+            send.at[stage, index],
+            recv.at[stage, index],
+            copy,
+            peer,
+        )
+
+    def arrived_across(kind, index):
+        weight_copy(0, kind, index).wait_recv()
+        weight_copy(1, kind, index).start()
+        weight_copy(2, kind, index).start()
+
+    def arrived_along(kind, index):
+        weight_copy(1, kind, index).wait_recv()
+        weight_copy(3, kind, index).start()
+
+    def each(count, step, start=0):
         def body(index, carry):
             step(index)
             return carry
 
-        lax.fori_loop(0, count, body, 0)
+        lax.fori_loop(start, count, body, 0)
 
     loads = [
         pltpu.make_async_copy(source, target, load_sem.at[index])
@@ -348,6 +367,7 @@
                 (ids_hbm, ids_ref),
                 (weights_hbm, weights_ref),
                 (modality_hbm, modality_ref),
+                (tokens_hbm, tokens),
                 (gain_hbm, gain_ref),
                 (gate_hbm, gate),
                 (up_hbm, up),
@@ -355,39 +375,33 @@
             )
         )
     ]
-
-    def token_load(block):
-        rows = part_rows(block)
-        return pltpu.make_async_copy(tokens_hbm.at[rows], tokens.at[rows], token_sem.at[block])
-
-    each(blocks, lambda block: token_load(block).start())
-    for load in loads[:4]:
+    for load in loads[:5]:
         load.start()
     barrier = pltpu.get_barrier_semaphore()
-    for peer in (first, second):
+    for copy, peer in ((copy_of, beside), (copy_of, above), (other_layer, me), (other_core, me)):
         pl.semaphore_signal(
-            barrier, inc=1, device_id={AXIS: peer}, device_id_type=pl.DeviceIdType.MESH
-        )
-    pl.semaphore_wait(barrier, 2)
-
-    def leave(block):
-        token_load(block).wait()
-        dense(block).start()
-
-    each(blocks, leave)
-    for load in loads[4:]:
-        load.start()
-    for load in loads[:4]:
+            barrier,
+            inc=1,
+            device_id={"dp": copy, AXIS: peer},
+            device_id_type=pl.DeviceIdType.MESH,
+        )
+    for load in loads[:3]:
         load.wait()
 
     lines = 8
     expert = lax.broadcasted_iota(jnp.int32, (lines, tok_rows), 0)
     named = jnp.zeros((lines, tok_rows), jnp.float32)
-    share = jnp.zeros((lines, tok_rows), jnp.float32)
+    share = jnp.where(
+        expert == devices,
+        jnp.broadcast_to(modality_ref[...].astype(jnp.float32), (lines, tok_rows)),
+        0.0,
+    )
+    late = jnp.zeros((1, tok_rows), jnp.float32)
     for k in range(fanout):
-        hit = expert == ids_ref[k : k + 1, :]
-        named = jnp.where(hit, 1.0, named)
-        share = jnp.where(hit, weights_ref[k : k + 1, :], share)
+        share = jnp.where(expert == ids_ref[k : k + 1, :], weights_ref[k : k + 1, :], share)
+        late = jnp.where(ids_ref[k : k + 1, :] == diagonal, 1.0, late)
+    facts[...] = share
+    named = jnp.where(expert == 0, late, 1.0 - late)
     before = (
         lax.broadcasted_iota(jnp.int32, (tok_rows, tok_rows), 0)
         < lax.broadcasted_iota(jnp.int32, (tok_rows, tok_rows), 1)
@@ -397,153 +411,199 @@
         jnp.where(before, 1.0, 0.0).astype(jnp.bfloat16),
         preferred_element_type=jnp.float32,
     )
-    facts[0:lines, :] = jnp.where(named > 0.5, count, -1.0)
-    facts[lines : 2 * lines, :] = share
-    facts[2 * lines : 3 * lines, :] = jnp.broadcast_to(
-        modality_ref[...].astype(jnp.float32), (lines, tok_rows)
-    )
-    told = remote(facts, near_facts, facts_sem.at[0], facts_sem.at[1], first)
+    slots[...] = jnp.broadcast_to(
+        jnp.where(late > 0.5, tok_rows - 1.0 - count[0:1, :], count[1:2, :]), (lines, tok_rows)
+    )
+
+    def sort(block):
+        slot = lax.broadcasted_iota(jnp.int32, (part, tok_rows), 0) + block * part
+        pick = jnp.where(slots[0:1, :] == slot.astype(jnp.float32), 1.0, 0.0).astype(jnp.bfloat16)
+        sorted_tokens[part_rows(block)] = jnp.dot(
+            pick, tokens[...], preferred_element_type=jnp.float32
+        ).astype(jnp.bfloat16)
+
+    loads[3].wait()
+    for load in loads[5:]:
+        load.start()
+    sort(0)
+    pl.semaphore_wait(barrier, 4)
+    dense(0).start()
+    each(groups, lambda index: [weight_copy(0, kind, index).start() for kind in range(2)])
+    each(pieces, lambda index: weight_copy(0, 2, index).start())
+
+    def leave(block):
+        sort(block)
+        dense(block).start()
+
+    each(blocks, leave, 1)
+
+    def keep(place, line):
+        columns[place] = jnp.broadcast_to(line, (LANES, tok_rows)).T
+
+    own_mine, own_far, near_mine, near_far, near_image, own_image, own_slot = range(7)
+    keep(own_slot, slots[0:1, :])
+    keep(own_mine, facts[pl.ds(me, 1), :])
+    keep(own_far, facts[pl.ds(above, 1), :])
+    keep(own_image, facts[devices : devices + 1, :])
+
+    def places(start, count):
+        slot = lax.broadcasted_iota(jnp.int32, (tok_rows, count), 1) + start
+        here = columns[own_slot, :, 0:1] == slot.astype(jnp.float32)
+        return jnp.where(here, 1.0, 0.0).astype(jnp.bfloat16)
+
+    coarse = share.astype(jnp.bfloat16)
+    fine = (share - coarse.astype(jnp.float32)).astype(jnp.bfloat16)
+    every = places(0, tok_rows)
+    sorted_facts[...] = jnp.dot(coarse, every, preferred_element_type=jnp.float32) + jnp.dot(
+        fine, every, preferred_element_type=jnp.float32
+    )
+    told = remote(sorted_facts, near_facts, facts_sem.at[0], facts_sem.at[1], copy_of, beside)
     told.start()
 
-    def column(line):
-        return jnp.broadcast_to(line, (LANES, tok_rows)).T[:, :1]
-
-    def normalize_rows(source, target, image, start, rows):
-        values = source[start : start + rows, :].astype(jnp.float32)
+    def normalize(source, target, image, rows):
+        values = source[rows, :].astype(jnp.float32)
         square = jnp.mean(values * values, axis=1, keepdims=True)
-        gains = jnp.where(
-            image[start : start + rows] > 0.5, gain_ref[1:2, :], gain_ref[0:1, :]
-        )
-        target[start : start + rows, :] = (
-            values * lax.rsqrt(square + epsilon) * gains
-        ).astype(jnp.bfloat16)
-
-    def pack(notes, rows, who, wave):
-        line = notes[pl.ds(who, 1), :]
-        slot = lax.broadcasted_iota(jnp.int32, (chunk, tok_rows), 0) + wave * chunk
-        pick = jnp.where(line == slot.astype(jnp.float32), 1.0, 0.0).astype(jnp.bfloat16)
-        return jnp.dot(pick, rows[...], preferred_element_type=jnp.float32).astype(jnp.bfloat16)
-
-    def feed(value):
-        opened = jnp.dot(value, gate[...], preferred_element_type=jnp.float32)
-        upper = jnp.dot(value, up[...], preferred_element_type=jnp.float32)
+        gains = jnp.where(image > 0.5, gain_ref[1:2, :], gain_ref[0:1, :])
+        target[rows, :] = (values * lax.rsqrt(square + epsilon) * gains).astype(jnp.bfloat16)
+
+    def feed(value, opening, upping, closing):
+        opened = jnp.dot(value, opening[...], preferred_element_type=jnp.float32)
+        upper = jnp.dot(value, upping[...], preferred_element_type=jnp.float32)
         active = (opened / (1.0 + jnp.exp(-opened)) * upper).astype(jnp.bfloat16)
-        return jnp.dot(active, down[...], preferred_element_type=jnp.float32).astype(jnp.bfloat16)
-
-    def spots(notes, who):
-        line = column(notes[pl.ds(who, 1), :])
-        worth = column(notes[pl.ds(who + lines, 1), :])
-        slot = lax.broadcasted_iota(jnp.int32, (tok_rows, capacity), 1)
-        full = jnp.where(line == slot.astype(jnp.float32), worth, 0.0)
-        coarse = full.astype(jnp.bfloat16)
-        return coarse, (full - coarse.astype(jnp.float32)).astype(jnp.bfloat16)
-
-    def spread(coarse, fine, value):
-        return jnp.dot(coarse, value, preferred_element_type=jnp.float32) + jnp.dot(
-            fine, value, preferred_element_type=jnp.float32
-        )
-
-    image = column(facts[2 * lines : 2 * lines + 1, :])
+        result = jnp.dot(active, closing[...], preferred_element_type=jnp.float32)
+        return result.astype(jnp.bfloat16).astype(jnp.float32)
+
+    loads[4].wait()
     rows = 64
-    for start in range(0, tok_rows, rows):
-        normalize_rows(tokens, normed, image, start, rows)
-
-    def send(wave):
-        packed[0, wave_rows(wave)] = pack(facts, normed, second, wave)
-        go(0, wave).start()
-
-    each(waves, send)
-
-    for load in loads[4:]:
+
+    def ready(index):
+        here = pl.ds(pl.multiple_of(index * rows, rows), rows)
+        normalize(tokens, normed, columns[own_image, here, 0:1], here)
+
+    each(tok_rows // rows, ready)
+    for load in loads[5:]:
         load.wait()
 
-    def local(wave):
-        here = wave_rows(wave)
-        own_results[here] = feed(pack(facts, normed, me, wave))
-
-    each(waves, local)
-    total[...] = tokens[...].astype(jnp.float32) + spread(*spots(facts, me), own_results[...])
-
-    def serve(kind, now):
-        def step(wave):
-            here = wave_rows(wave)
-            go(kind, wave).wait_recv()
-            finished[kind, here] = feed(arrived[kind, here])
-
-            @pl.when(wave < now)
+    batch = tok_rows // groups
+
+    def batch_rows(group):
+        return pl.ds(pl.multiple_of(group * batch, batch), batch)
+
+    told.wait_recv()
+    keep(near_mine, near_facts[pl.ds(me, 1), :])
+    keep(near_far, near_facts[pl.ds(above, 1), :])
+    keep(near_image, near_facts[devices : devices + 1, :])
+
+    def both(group):
+        here = batch_rows(group)
+        total[here, :] = tokens[here, :].astype(jnp.float32) + columns[own_mine, here, 0:1] * feed(
+            normed[here, :], gate, up, down
+        )
+        arrived_across(0, group)
+
+        @pl.when(group > 0)
+        def _():
+            arrived_along(1, group - 1)
+
+        arrived_across(1, group)
+        for index in range(blocks // groups):
+            dense(group * (blocks // groups) + index).wait_recv()
+        for start in range(0, batch, rows):
+            few = pl.ds(pl.multiple_of(group * batch + start, rows), rows)
+            normalize(near_tokens, near_normed, columns[near_image, few, 0:1], few)
+        near = columns[near_mine, here, 0:1] * feed(near_normed[here, :], gate, up, down)
+        near_total[here, :] = near
+        sum_out[here, :] = near.astype(jnp.bfloat16)
+        for index in range(blocks // groups):
+            block = group * (blocks // groups) + index
+
+            @pl.when(block < free)
             def _():
-                back(kind, wave).start()
-
-        each(waves, step)
-
-    serve(0, waves - 1)
-
-    told.wait_recv()
-    near_image = column(near_facts[2 * lines : 2 * lines + 1, :])
-    for block in range(blocks):
-        dense(block).wait_recv()
-        for start in range(block * part, (block + 1) * part, rows):
-            normalize_rows(near_tokens, near_normed, near_image, start, rows)
-
-    def forward(wave):
-        packed[1, wave_rows(wave)] = pack(near_facts, near_normed, second, wave)
-        go(1, wave).start()
-
-    each(waves, forward)
-
-    def near_local(wave):
-        here = wave_rows(wave)
-        own_rows[here] = feed(pack(near_facts, near_normed, me, wave))
-
-    each(waves, near_local)
-    near_total[...] = spread(*spots(near_facts, me), own_rows[...])
-
-    serve(1, waves)
-    back(0, waves - 1).start()
-
-    coarse, fine = spots(near_facts, second)
-    each(waves, lambda wave: back(1, wave).wait_recv())
-    for block in range(blocks):
-        here = slice(block * part, (block + 1) * part)
-        sum_out[here, :] = (
-            near_total[here, :] + spread(coarse[here], fine[here], returned[1])
-        ).astype(jnp.bfloat16)
+                sums(block).start()
+
+        arrived_along(0, group)
+
+    each(groups, both)
+
+    def close(index):
+        arrived_across(2, index)
+
+        @pl.when(index == 0)
+        def _():
+            arrived_along(1, groups - 1)
+
+        @pl.when(index > 0)
+        def _():
+            arrived_along(2, index - 1)
+
+    each(pieces, close)
+    arrived_along(2, pieces - 1)
+
+    def joined(kind, index):
+        weight_copy(2, kind, index).wait_recv()
+        weight_copy(3, kind, index).wait_recv()
+
+    each(groups, lambda index: [joined(kind, index) for kind in range(2)])
+    each(pieces, lambda index: joined(2, index))
+
+    def finish(block):
+        here = part_rows(block)
+        near = near_total[here, :] + columns[near_far, here, 0:1] * feed(
+            near_normed[here, :], far_gate, far_up, far_down
+        )
+        sum_out[here, :] = near.astype(jnp.bfloat16)
         sums(block).start()
 
-    each(waves, lambda wave: back(0, wave).wait_recv())
-    total[...] += spread(*spots(facts, second), returned[0])
-
-    for block in range(blocks):
-        here = slice(block * part, (block + 1) * part)
+    each(blocks, finish, free)
+
+    def own(group):
+        here = batch_rows(group)
+        total[here, :] += columns[own_far, here, 0:1] * feed(
+            normed[here, :], far_gate, far_up, far_down
+        )
+
+    each(groups, own)
+
+    def take(block):
         sums(block).wait_recv()
-        out_ref[here, :] = (total[here, :] + sum_in[here, :].astype(jnp.float32)).astype(
-            out_ref.dtype
-        )
+        return jnp.dot(
+            places(block * part, part), sum_in[part_rows(block)], preferred_element_type=jnp.float32
+        )
+
+    def collect(block):
+        total[...] += take(block)
+
+    each(blocks - 1, collect)
+    out_ref[...] = (total[...] + take(blocks - 1)).astype(out_ref.dtype)
 
     told.wait_send()
     each(blocks, lambda block: dense(block).wait_send())
     each(blocks, lambda block: sums(block).wait_send())
-    for kind in range(2):
-        each(waves, lambda wave: go(kind, wave).wait_send())
-        each(waves, lambda wave: back(kind, wave).wait_send())
-
-
-def relay_scratch(tok_rows, width, hidden, fanout, capacity, waves, blocks):
+
+    def sent(kind, index):
+        for stage in range(4):
+            weight_copy(stage, kind, index).wait_send()
+
+    each(groups, lambda index: [sent(kind, index) for kind in range(2)])
+    each(pieces, lambda index: sent(2, index))
+
+
+def pair_scratch(tok_rows, width, hidden, fanout, blocks, groups, pieces):
     dense = pltpu.VMEM((tok_rows, width), jnp.bfloat16)
     sums = pltpu.VMEM((tok_rows, width), jnp.float32)
-    facts = pltpu.VMEM((24, tok_rows), jnp.float32)
-    slots = pltpu.VMEM((2, capacity, width), jnp.bfloat16)
-    single = pltpu.VMEM((capacity, width), jnp.bfloat16)
+    facts = pltpu.VMEM((8, tok_rows), jnp.float32)
     wide = pltpu.VMEM((width, hidden), jnp.bfloat16)
+    tall = pltpu.VMEM((hidden, width), jnp.bfloat16)
     by_block = pltpu.SemaphoreType.DMA((blocks,))
-    by_wave = pltpu.SemaphoreType.DMA((2, waves))
+    by_group = pltpu.SemaphoreType.DMA((2, 4, groups))
+    by_piece = pltpu.SemaphoreType.DMA((4, pieces))
     return [
         pltpu.VMEM((1, tok_rows), jnp.int32), pltpu.VMEM((fanout, tok_rows), jnp.int32),
         pltpu.VMEM((fanout, tok_rows), jnp.float32), pltpu.VMEM((2, width), jnp.float32),
-        dense, dense, wide, wide, pltpu.VMEM((hidden, width), jnp.bfloat16), dense, dense,
-        sums, sums, facts, facts, slots, slots, slots, slots, single, single, dense, dense,
-        pltpu.SemaphoreType.DMA((7,)), by_block, pltpu.SemaphoreType.DMA((2,)), by_block, by_block,
-        by_wave, by_wave, by_wave, by_wave, by_block, by_block,
+        dense, dense, dense, wide, wide, tall, wide, wide, tall, dense, dense, sums, sums,
+        facts, facts, facts, facts, pltpu.VMEM((7, tok_rows, LANES), jnp.float32), dense, dense,
+        pltpu.SemaphoreType.DMA((8,)), pltpu.SemaphoreType.DMA((2,)),
+        by_block, by_block, by_block, by_block, by_group, by_group, by_piece, by_piece,
     ]
 
 
@@ -584,22 +644,29 @@
     near = pl.BlockSpec(memory_space=pltpu.VMEM)
     far = pl.BlockSpec(memory_space=pl.ANY)
     sems = pltpu.SemaphoreType.DMA((waves, devices))
-    blocks = 4
-    relayed = devices == 4 and tok_rows % (64 * blocks) == 0 and capacity % 32 == 0
-    if relayed:
-        kernel = functools.partial(relay_kernel, blocks)
-        scratch = relay_scratch(tok_rows, width, hidden, fanout, capacity, 2, blocks)
+    blocks, groups, pieces = 8, 4, hidden // 128
+    paired = (
+        devices == 4
+        and lax.axis_size("dp") % 4 == 0
+        and tok_rows % (LANES * groups) == 0
+        and tok_rows % (64 * blocks) == 0
+        and width % (64 * groups) == 0
+        and hidden % 128 == 0
+    )
+    if paired:
+        kernel = functools.partial(pair_kernel, blocks, groups, pieces)
+        scratch = pair_scratch(tok_rows, width, hidden, fanout, blocks, groups, pieces)
     else:
         kernel = functools.partial(moe_kernel, devices)
         scratch = direct_scratch(tok_rows, width, hidden, buffer, sems)
     return pl.pallas_call(
         kernel,
         out_shape=pltpu.VMEM((tok_rows, width), jnp.bfloat16),
-        in_specs=[far] + [far if relayed else near] * 4 + [far] * 3,
+        in_specs=[far] + [far if paired else near] * 4 + [far] * 3,
         out_specs=near,
         scratch_shapes=scratch,
         compiler_params=pltpu.CompilerParams(
-            collective_id=0, has_side_effects=True, vmem_limit_bytes=58 * 1024 * 1024
+            collective_id=0, has_side_effects=True, vmem_limit_bytes=(60 if paired else 58) * 1024 * 1024
         ),
     )(
         tokens,

time: 114 us -> 150 us (1.32); the launches traced: 111 us -> 149 us
  Pallas kernels: 110 us -> 148 us
    pallas_call x1, Pallas kernels: 110 us -> 148 us  [shards(): pl.pallas_call(kernel, out_shape=pltpu.VMEM((tok_rows, width), jnp.bfloat...]
where the time goes in v1:
time: 150 us; the launch traced here: 149 us
  Pallas kernels  148 us (99%)
    pallas_call x1, Pallas kernels, shards(): pl.pallas_call(kernel, out_shape=pltpu.VMEM((tok_rows, width), jnp.bfloat...  148 us

profile of v1, /device:TPU:0, one launch (start us, length us, event | category | flops | bytes accessed | tf_op | source)
XLA Modules:
  0.0 149.3 jit_solution(1048400247818483750)
XLA Ops:
  0.0 148.0 %shard_map.82 = bf16[512,2048]{1,0:T(8,128)(2,1)S(1)} custom-call(bf16[512,2048]{1,0:T(8,128)(2,1)} %tokens_hbm.1, s32[1,512]{1,0:T(1,128)} %bitcast.5, s32[2,512]{1,0:T(2,128)} %bitcast.3, f32[2,512]{1,0:T(2,128)} %bitcast.4, f32[2,2048]{1,0:T(2,128)} %gain_hbm.1, bf16[2048,896]{1,0:T(8,128)(2,1)} %gate_hbm.1, bf16[2048,896]{1,0:T(8,128)(2,1)} %up_hbm.1, ...), custom_call_target="tpu_custom_call" | custom-call | tf_op jit(solution)/shard_map/pallas_call | solution.py:662
  148.0 1.3 copy.10

commit v2 on v1

--- a/solution.py
+++ b/solution.py
@@ -261,6 +261,7 @@
     near_facts,
     slots,
     columns,
+    active,
     sum_out,
     sum_in,
     load_sem,
@@ -319,25 +320,46 @@
     def sums(block):
         rows = part_rows(block)
         return remote(
-            sum_out.at[rows], sum_in.at[rows], sum_send.at[block], sum_recv.at[block], copy_of, beside
+            sum_out.at[rows],
+            sum_in.at[rows],
+            sum_send.at[0, block],
+            sum_recv.at[0, block],
+            copy_of,
+            beside,
+        )
+
+    half = width // 2
+    halves = (pl.ds(0, half), pl.ds(half, half))
+
+    def late_sums(side, block):
+        rows = part_rows(block)
+        return remote(
+            sum_out.at[rows, halves[side]],
+            sum_in.at[rows, halves[side]],
+            sum_send.at[side, block],
+            sum_recv.at[side, block],
+            copy_of,
+            beside,
         )
 
     wide_rows = width // 4 // groups
     tall_rows = hidden // 4 // pieces
 
     def weight_copy(stage, kind, index):
+        which = layer_quarter if stage == 3 else quarter
         if kind < 2:
             near, far = ((gate_hbm, far_gate), (up_hbm, far_up))[kind]
-            count, whole, send, recv = wide_rows, width // 4, wide_send.at[kind], wide_recv.at[kind]
+            send, recv = wide_send.at[kind], wide_recv.at[kind]
+            start = which * (width // 4) + index * wide_rows
+            spot = (pl.ds(pl.multiple_of(start, wide_rows), wide_rows),)
         else:
-            near, far = down_hbm, far_down
-            count, whole, send, recv = tall_rows, hidden // 4, tall_send, tall_recv
-        which = layer_quarter if stage == 3 else quarter
-        rows = pl.ds(pl.multiple_of(which * whole + index * count, count), count)
+            near, far, send, recv = down_hbm, far_down, tall_send, tall_recv
+            start = which * (hidden // 4) + index % pieces * tall_rows
+            spot = (pl.ds(pl.multiple_of(start, tall_rows), tall_rows), halves[index // pieces])
         copy, peer = ((copy_of, above), (other_layer, me), (other_core, me), (other_core, me))[stage]
         return remote(
-            (near if stage == 0 else far).at[rows],
-            far.at[rows],
+            (near if stage == 0 else far).at[spot],
+            far.at[spot],
             send.at[stage, index],
             recv.at[stage, index],
             copy,
@@ -429,13 +451,8 @@
     pl.semaphore_wait(barrier, 4)
     dense(0).start()
     each(groups, lambda index: [weight_copy(0, kind, index).start() for kind in range(2)])
-    each(pieces, lambda index: weight_copy(0, 2, index).start())
-
-    def leave(block):
-        sort(block)
-        dense(block).start()
-
-    each(blocks, leave, 1)
+    for index in range(2 * pieces):
+        weight_copy(0, 2, index).start()
 
     def keep(place, line):
         columns[place] = jnp.broadcast_to(line, (LANES, tok_rows)).T
@@ -460,18 +477,29 @@
     told = remote(sorted_facts, near_facts, facts_sem.at[0], facts_sem.at[1], copy_of, beside)
     told.start()
 
+    def leave(block):
+        sort(block)
+        dense(block).start()
+
+    each(blocks, leave, 1)
+
     def normalize(source, target, image, rows):
         values = source[rows, :].astype(jnp.float32)
         square = jnp.mean(values * values, axis=1, keepdims=True)
         gains = jnp.where(image > 0.5, gain_ref[1:2, :], gain_ref[0:1, :])
         target[rows, :] = (values * lax.rsqrt(square + epsilon) * gains).astype(jnp.bfloat16)
 
-    def feed(value, opening, upping, closing):
+    def activate(value, opening, upping):
         opened = jnp.dot(value, opening[...], preferred_element_type=jnp.float32)
         upper = jnp.dot(value, upping[...], preferred_element_type=jnp.float32)
-        active = (opened / (1.0 + jnp.exp(-opened)) * upper).astype(jnp.bfloat16)
-        result = jnp.dot(active, closing[...], preferred_element_type=jnp.float32)
+        return (opened / (1.0 + jnp.exp(-opened)) * upper).astype(jnp.bfloat16)
+
+    def settle(value, closing):
+        result = jnp.dot(value, closing, preferred_element_type=jnp.float32)
         return result.astype(jnp.bfloat16).astype(jnp.float32)
+
+    def feed(value, opening, upping, closing):
+        return settle(activate(value, opening, upping), closing[...])
 
     loads[4].wait()
     rows = 64
@@ -489,25 +517,41 @@
     def batch_rows(group):
         return pl.ds(pl.multiple_of(group * batch, batch), batch)
 
-    told.wait_recv()
-    keep(near_mine, near_facts[pl.ds(me, 1), :])
-    keep(near_far, near_facts[pl.ds(above, 1), :])
-    keep(near_image, near_facts[devices : devices + 1, :])
+    double = 2 * batch
+
+    def pair_rows(group):
+        return pl.ds(pl.multiple_of(group * double, double), double)
 
     def both(group):
-        here = batch_rows(group)
-        total[here, :] = tokens[here, :].astype(jnp.float32) + columns[own_mine, here, 0:1] * feed(
-            normed[here, :], gate, up, down
-        )
         arrived_across(0, group)
+
+        @pl.when(group < tok_rows // double)
+        def _():
+            here = pair_rows(group)
+            total[here, :] = tokens[here, :].astype(jnp.float32) + columns[
+                own_mine, here, 0:1
+            ] * feed(normed[here, :], gate, up, down)
 
         @pl.when(group > 0)
         def _():
             arrived_along(1, group - 1)
 
         arrived_across(1, group)
+
+        @pl.when(group == 0)
+        def _():
+            told.wait_recv()
+            keep(near_mine, near_facts[pl.ds(me, 1), :])
+            keep(near_far, near_facts[pl.ds(above, 1), :])
+            keep(near_image, near_facts[devices : devices + 1, :])
+
+        @pl.when(group == groups - 1)
+        def _():
+            arrived_across(2, 0)
+
         for index in range(blocks // groups):
             dense(group * (blocks // groups) + index).wait_recv()
+        here = batch_rows(group)
         for start in range(0, batch, rows):
             few = pl.ds(pl.multiple_of(group * batch + start, rows), rows)
             normalize(near_tokens, near_normed, columns[near_image, few, 0:1], few)
@@ -524,71 +568,86 @@
         arrived_along(0, group)
 
     each(groups, both)
-
-    def close(index):
-        arrived_across(2, index)
-
-        @pl.when(index == 0)
-        def _():
-            arrived_along(1, groups - 1)
-
-        @pl.when(index > 0)
-        def _():
-            arrived_along(2, index - 1)
-
-    each(pieces, close)
-    arrived_along(2, pieces - 1)
+    arrived_along(1, groups - 1)
+    arrived_across(2, 1)
 
     def joined(kind, index):
         weight_copy(2, kind, index).wait_recv()
         weight_copy(3, kind, index).wait_recv()
 
+    late = slice(free * part, tok_rows)
     each(groups, lambda index: [joined(kind, index) for kind in range(2)])
-    each(pieces, lambda index: joined(2, index))
-
-    def finish(block):
-        here = part_rows(block)
-        near = near_total[here, :] + columns[near_far, here, 0:1] * feed(
-            near_normed[here, :], far_gate, far_up, far_down
-        )
-        sum_out[here, :] = near.astype(jnp.bfloat16)
-        sums(block).start()
-
-    each(blocks, finish, free)
+    active[...] = activate(near_normed[late, :], far_gate, far_up)
+
+    def finish(side):
+        for index in range(side * pieces, (side + 1) * pieces):
+            joined(2, index)
+        there = slice(side * half, (side + 1) * half)
+        sum_out[late, there] = (
+            near_total[late, there]
+            + columns[near_far, late, 0:1] * settle(active[...], far_down[:, there])
+        ).astype(jnp.bfloat16)
+        each(blocks, lambda block: late_sums(side, block).start(), free)
+
+    arrived_along(2, 0)
+    arrived_across(2, 2)
+    arrived_along(2, 1)
+    finish(0)
+    arrived_across(2, 3)
+    arrived_along(2, 2)
+    each(free, lambda block: sums(block).wait_recv())
+    total[...] += jnp.dot(
+        places(0, free * part), sum_in[: free * part, :], preferred_element_type=jnp.float32
+    )
+    arrived_along(2, 3)
+    finish(1)
 
     def own(group):
-        here = batch_rows(group)
+        here = pair_rows(group)
         total[here, :] += columns[own_far, here, 0:1] * feed(
             normed[here, :], far_gate, far_up, far_down
         )
 
-    each(groups, own)
-
-    def take(block):
-        sums(block).wait_recv()
-        return jnp.dot(
-            places(block * part, part), sum_in[part_rows(block)], preferred_element_type=jnp.float32
-        )
-
-    def collect(block):
-        total[...] += take(block)
-
-    each(blocks - 1, collect)
-    out_ref[...] = (total[...] + take(blocks - 1)).astype(out_ref.dtype)
+    each(tok_rows // double, own)
+
+    def take(side, first, last):
+        each(last, lambda block: late_sums(side, block).wait_recv(), first)
+        there = slice(side * half, (side + 1) * half)
+        some = slice(first * part, last * part)
+        out_ref[:, there] = (
+            total[:, there]
+            + jnp.dot(
+                places(first * part, (last - first) * part),
+                sum_in[some, there],
+                preferred_element_type=jnp.float32,
+            )
+        ).astype(out_ref.dtype)
+
+    take(0, free, blocks)
+    each(blocks - 1, lambda block: late_sums(1, block).wait_recv(), free)
+    total[:, half:] += jnp.dot(
+        places(free * part, (blocks - 1 - free) * part),
+        sum_in[free * part : (blocks - 1) * part, half:],
+        preferred_element_type=jnp.float32,
+    )
+    take(1, blocks - 1, blocks)
 
     told.wait_send()
     each(blocks, lambda block: dense(block).wait_send())
-    each(blocks, lambda block: sums(block).wait_send())
+    each(free, lambda block: sums(block).wait_send())
+    for side in range(2):
+        each(blocks, lambda block: late_sums(side, block).wait_send(), free)
 
     def sent(kind, index):
         for stage in range(4):
             weight_copy(stage, kind, index).wait_send()
 
     each(groups, lambda index: [sent(kind, index) for kind in range(2)])
-    each(pieces, lambda index: sent(2, index))
-
-
-def pair_scratch(tok_rows, width, hidden, fanout, blocks, groups, pieces):
+    for index in range(2 * pieces):
+        sent(2, index)
+
+
+def pair_scratch(tok_rows, width, hidden, fanout, capacity, blocks, groups, pieces):
     dense = pltpu.VMEM((tok_rows, width), jnp.bfloat16)
     sums = pltpu.VMEM((tok_rows, width), jnp.float32)
     facts = pltpu.VMEM((8, tok_rows), jnp.float32)
@@ -596,14 +655,18 @@
     tall = pltpu.VMEM((hidden, width), jnp.bfloat16)
     by_block = pltpu.SemaphoreType.DMA((blocks,))
     by_group = pltpu.SemaphoreType.DMA((2, 4, groups))
-    by_piece = pltpu.SemaphoreType.DMA((4, pieces))
+    by_piece = pltpu.SemaphoreType.DMA((4, 2 * pieces))
+    by_side = pltpu.SemaphoreType.DMA((2, blocks))
+    part = tok_rows // blocks
+    late = tok_rows - (tok_rows - capacity) // part * part
     return [
         pltpu.VMEM((1, tok_rows), jnp.int32), pltpu.VMEM((fanout, tok_rows), jnp.int32),
         pltpu.VMEM((fanout, tok_rows), jnp.float32), pltpu.VMEM((2, width), jnp.float32),
         dense, dense, dense, wide, wide, tall, wide, wide, tall, dense, dense, sums, sums,
-        facts, facts, facts, facts, pltpu.VMEM((7, tok_rows, LANES), jnp.float32), dense, dense,
+        facts, facts, facts, facts, pltpu.VMEM((7, tok_rows, LANES), jnp.float32),
+        pltpu.VMEM((late, hidden), jnp.bfloat16), dense, dense,
         pltpu.SemaphoreType.DMA((8,)), pltpu.SemaphoreType.DMA((2,)),
-        by_block, by_block, by_block, by_block, by_group, by_group, by_piece, by_piece,
+        by_block, by_block, by_side, by_side, by_group, by_group, by_piece, by_piece,
     ]
 
 
@@ -644,7 +707,7 @@
     near = pl.BlockSpec(memory_space=pltpu.VMEM)
     far = pl.BlockSpec(memory_space=pl.ANY)
     sems = pltpu.SemaphoreType.DMA((waves, devices))
-    blocks, groups, pieces = 8, 4, hidden // 128
+    blocks, groups, pieces = 8, 4, 2
     paired = (
         devices == 4
         and lax.axis_size("dp") % 4 == 0
@@ -655,7 +718,7 @@
     )
     if paired:
         kernel = functools.partial(pair_kernel, blocks, groups, pieces)
-        scratch = pair_scratch(tok_rows, width, hidden, fanout, blocks, groups, pieces)
+        scratch = pair_scratch(tok_rows, width, hidden, fanout, capacity, blocks, groups, pieces)
     else:
         kernel = functools.partial(moe_kernel, devices)
         scratch = direct_scratch(tok_rows, width, hidden, buffer, sems)

time: 150 us -> 99.6 us (0.66)
  Pallas kernels: 148 us -> 98.1 us
    pallas_call x1, Pallas kernels: 148 us -> 98.1 us  [shards(): pl.pallas_call(kernel, out_shape=pltpu.VMEM((tok_rows, width), jnp.bfloat...]
where the time goes in v2:
time: 99.6 us; the launch traced here: 99.4 us
  Pallas kernels  98.1 us (98%)
  local copies, waits for them, and re-layouts  1.32 us (1%)
    pallas_call x1, Pallas kernels, shards(): pl.pallas_call(kernel, out_shape=pltpu.VMEM((tok_rows, width), jnp.bfloat...  98.1 us

profile of v2, /device:TPU:0, one launch (start us, length us, event | category | flops | bytes accessed | tf_op | source)
XLA Modules:
  0.0 99.4 jit_solution(9356366830660886540)
XLA Ops:
  0.0 98.1 %shard_map.82 = bf16[512,2048]{1,0:T(8,128)(2,1)S(1)} custom-call(bf16[512,2048]{1,0:T(8,128)(2,1)} %tokens_hbm.1, s32[1,512]{1,0:T(1,128)} %bitcast.5, s32[2,512]{1,0:T(2,128)} %bitcast.3, f32[2,512]{1,0:T(2,128)} %bitcast.4, f32[2,2048]{1,0:T(2,128)} %gain_hbm.1, bf16[2048,896]{1,0:T(8,128)(2,1)} %gate_hbm.1, bf16[2048,896]{1,0:T(8,128)(2,1)} %up_hbm.1, ...), custom_call_target="tpu_custom_call" | custom-call | tf_op jit(solution)/shard_map/pallas_call | solution.py:725
  98.1 1.3 %copy.10 = bf16[512,2048]{1,0:T(8,128)(2,1)} copy(bf16[512,2048]{1,0:T(8,128)(2,1)S(1)} %shard_map.82) | data formatting | bytes 4194304

commit v3 on v2

--- a/solution.py
+++ b/solution.py
@@ -229,7 +229,7 @@
 def pair_kernel(
     blocks,
     groups,
-    pieces,
+    sides,
     tokens_hbm,
     modality_hbm,
     ids_hbm,
@@ -262,6 +262,8 @@
     slots,
     columns,
     active,
+    own_active,
+    relayed,
     sum_out,
     sum_in,
     load_sem,
@@ -274,6 +276,10 @@
     wide_recv,
     tall_send,
     tall_recv,
+    out_send,
+    out_recv,
+    home_send,
+    home_recv,
 ):
     tok_rows, width = tokens.shape
     hidden = gate.shape[1]
@@ -287,9 +293,13 @@
     layer, core = copy_of // 2, copy_of % 2
     beside = me // 2 * 2 + 1 - me % 2
     above = (1 - me // 2) * 2 + me % 2
+    kind_of = layer // 2 % 2
+    first = beside * (1 - kind_of) + above * kind_of
+    second = above * (1 - kind_of) + beside * kind_of
     diagonal = (1 - me // 2) * 2 + 1 - me % 2
     other_layer = (layer // 2 * 2 + 1 - layer % 2) * 2 + core
     other_core = layer * 2 + 1 - core
+    far_layer = (layer // 4 * 4 + (layer + 2) % 4) * 2 + core
     quarter = layer % 2 * 2 + core
     layer_quarter = (1 - layer % 2) * 2 + core
 
@@ -314,7 +324,7 @@
             dense_send.at[block],
             dense_recv.at[block],
             copy_of,
-            beside,
+            first,
         )
 
     def sums(block):
@@ -325,28 +335,54 @@
             sum_send.at[0, block],
             sum_recv.at[0, block],
             copy_of,
-            beside,
-        )
-
-    half = width // 2
-    halves = (pl.ds(0, half), pl.ds(half, half))
+            first,
+        )
+
+    slim = width // sides
+
+    def columns_of(side):
+        return pl.ds(side * slim, slim)
 
     def late_sums(side, block):
         rows = part_rows(block)
         return remote(
-            sum_out.at[rows, halves[side]],
-            sum_in.at[rows, halves[side]],
+            sum_out.at[rows, columns_of(side)],
+            sum_in.at[rows, columns_of(side)],
             sum_send.at[side, block],
             sum_recv.at[side, block],
             copy_of,
-            beside,
+            first,
+        )
+
+    detours = blocks - free - 1
+
+    def out(index):
+        rows = part_rows(index)
+        return remote(
+            sum_out.at[part_rows(free + index), columns_of(0)],
+            relayed.at[rows],
+            out_send.at[index],
+            out_recv.at[index],
+            far_layer,
+            first,
+        )
+
+    def home(index):
+        rows = part_rows(index)
+        return remote(
+            relayed.at[rows],
+            sum_in.at[part_rows(free + index), columns_of(0)],
+            home_send.at[index],
+            home_recv.at[index],
+            far_layer,
+            me,
         )
 
     wide_rows = width // 4 // groups
-    tall_rows = hidden // 4 // pieces
+    tall_rows = hidden // 4
 
     def weight_copy(stage, kind, index):
-        which = layer_quarter if stage == 3 else quarter
+        which = layer_quarter if stage in (3, 4) else quarter
         if kind < 2:
             near, far = ((gate_hbm, far_gate), (up_hbm, far_up))[kind]
             send, recv = wide_send.at[kind], wide_recv.at[kind]
@@ -354,11 +390,17 @@
             spot = (pl.ds(pl.multiple_of(start, wide_rows), wide_rows),)
         else:
             near, far, send, recv = down_hbm, far_down, tall_send, tall_recv
-            start = which * (hidden // 4) + index % pieces * tall_rows
-            spot = (pl.ds(pl.multiple_of(start, tall_rows), tall_rows), halves[index // pieces])
-        copy, peer = ((copy_of, above), (other_layer, me), (other_core, me), (other_core, me))[stage]
+            start = which * tall_rows
+            spot = (pl.ds(pl.multiple_of(start, tall_rows), tall_rows), columns_of(index))
+        copy, peer = (
+            (copy_of, second),
+            (other_layer, me),
+            (other_core, me),
+            (other_core, me),
+            (copy_of, second),
+        )[stage]
         return remote(
-            (near if stage == 0 else far).at[spot],
+            (near if stage in (0, 4) else far).at[spot],
             far.at[spot],
             send.at[stage, index],
             recv.at[stage, index],
@@ -368,11 +410,12 @@
 
     def arrived_across(kind, index):
         weight_copy(0, kind, index).wait_recv()
-        weight_copy(1, kind, index).start()
+        if kind < 2 or index < sides - 1:
+            weight_copy(1, kind, index).start()
         weight_copy(2, kind, index).start()
 
     def arrived_along(kind, index):
-        weight_copy(1, kind, index).wait_recv()
+        weight_copy(1 if kind < 2 or index < sides - 1 else 4, kind, index).wait_recv()
         weight_copy(3, kind, index).start()
 
     def each(count, step, start=0):
@@ -397,16 +440,25 @@
             )
         )
     ]
-    for load in loads[:5]:
-        load.start()
     barrier = pltpu.get_barrier_semaphore()
-    for copy, peer in ((copy_of, beside), (copy_of, above), (other_layer, me), (other_core, me)):
+    partners = (
+        (far_layer, first),
+        (far_layer, second),
+        (far_layer, me),
+        (copy_of, first),
+        (copy_of, second),
+        (other_layer, me),
+        (other_core, me),
+    )
+    for copy, peer in partners:
         pl.semaphore_signal(
             barrier,
             inc=1,
             device_id={"dp": copy, AXIS: peer},
             device_id_type=pl.DeviceIdType.MESH,
         )
+    for load in loads[:5]:
+        load.start()
     for load in loads[:3]:
         load.wait()
 
@@ -448,11 +500,12 @@
     for load in loads[5:]:
         load.start()
     sort(0)
-    pl.semaphore_wait(barrier, 4)
+    pl.semaphore_wait(barrier, len(partners))
     dense(0).start()
     each(groups, lambda index: [weight_copy(0, kind, index).start() for kind in range(2)])
-    for index in range(2 * pieces):
-        weight_copy(0, 2, index).start()
+    for side in range(sides):
+        weight_copy(0, 2, side).start()
+    weight_copy(4, 2, sides - 1).start()
 
     def keep(place, line):
         columns[place] = jnp.broadcast_to(line, (LANES, tok_rows)).T
@@ -460,7 +513,7 @@
     own_mine, own_far, near_mine, near_far, near_image, own_image, own_slot = range(7)
     keep(own_slot, slots[0:1, :])
     keep(own_mine, facts[pl.ds(me, 1), :])
-    keep(own_far, facts[pl.ds(above, 1), :])
+    keep(own_far, facts[pl.ds(second, 1), :])
     keep(own_image, facts[devices : devices + 1, :])
 
     def places(start, count):
@@ -474,7 +527,7 @@
     sorted_facts[...] = jnp.dot(coarse, every, preferred_element_type=jnp.float32) + jnp.dot(
         fine, every, preferred_element_type=jnp.float32
     )
-    told = remote(sorted_facts, near_facts, facts_sem.at[0], facts_sem.at[1], copy_of, beside)
+    told = remote(sorted_facts, near_facts, facts_sem.at[0], facts_sem.at[1], copy_of, first)
     told.start()
 
     def leave(block):
@@ -542,7 +595,7 @@
         def _():
             told.wait_recv()
             keep(near_mine, near_facts[pl.ds(me, 1), :])
-            keep(near_far, near_facts[pl.ds(above, 1), :])
+            keep(near_far, near_facts[pl.ds(second, 1), :])
             keep(near_image, near_facts[devices : devices + 1, :])
 
         @pl.when(group == groups - 1)
@@ -580,74 +633,96 @@
     active[...] = activate(near_normed[late, :], far_gate, far_up)
 
     def finish(side):
-        for index in range(side * pieces, (side + 1) * pieces):
-            joined(2, index)
-        there = slice(side * half, (side + 1) * half)
+        joined(2, side)
+        there = slice(side * slim, (side + 1) * slim)
         sum_out[late, there] = (
             near_total[late, there]
             + columns[near_far, late, 0:1] * settle(active[...], far_down[:, there])
         ).astype(jnp.bfloat16)
-        each(blocks, lambda block: late_sums(side, block).start(), free)
+        if side == 0:
+            each(detours, lambda index: out(index).start())
+        each(blocks, lambda block: late_sums(side, block).start(), direct(side))
+
+    def direct(side):
+        return free + detours if side == 0 else free
+
+    def pass_on(index):
+        out(index).wait_recv()
+        home(index).start()
+
+    def own(group):
+        here = pair_rows(group)
+        own_active[here, :] = activate(normed[here, :], far_gate, far_up)
+
+    def own_finish(side):
+        there = slice(side * slim, (side + 1) * slim)
+        total[:, there] += columns[own_far, :, 0:1] * settle(own_active[...], far_down[:, there])
 
     arrived_along(2, 0)
+    finish(0)
     arrived_across(2, 2)
     arrived_along(2, 1)
-    finish(0)
+    finish(1)
+    own(0)
     arrived_across(2, 3)
     arrived_along(2, 2)
+    finish(2)
+    each(detours // 2, pass_on)
+    each(tok_rows // double, own, 1)
+    arrived_along(2, 3)
+    finish(3)
+    each(detours, pass_on, detours // 2)
     each(free, lambda block: sums(block).wait_recv())
     total[...] += jnp.dot(
         places(0, free * part), sum_in[: free * part, :], preferred_element_type=jnp.float32
     )
-    arrived_along(2, 3)
-    finish(1)
-
-    def own(group):
-        here = pair_rows(group)
-        total[here, :] += columns[own_far, here, 0:1] * feed(
-            normed[here, :], far_gate, far_up, far_down
-        )
-
-    each(tok_rows // double, own)
-
-    def take(side, first, last):
-        each(last, lambda block: late_sums(side, block).wait_recv(), first)
-        there = slice(side * half, (side + 1) * half)
-        some = slice(first * part, last * part)
-        out_ref[:, there] = (
-            total[:, there]
-            + jnp.dot(
-                places(first * part, (last - first) * part),
-                sum_in[some, there],
-                preferred_element_type=jnp.float32,
-            )
-        ).astype(out_ref.dtype)
-
-    take(0, free, blocks)
-    each(blocks - 1, lambda block: late_sums(1, block).wait_recv(), free)
-    total[:, half:] += jnp.dot(
-        places(free * part, (blocks - 1 - free) * part),
-        sum_in[free * part : (blocks - 1) * part, half:],
-        preferred_element_type=jnp.float32,
-    )
-    take(1, blocks - 1, blocks)
+    for side in range(sides):
+        own_finish(side)
+
+    def gathered(side, begin, end):
+        return total[:, side * slim : (side + 1) * slim] + jnp.dot(
+            places(begin * part, (end - begin) * part),
+            sum_in[begin * part : end * part, side * slim : (side + 1) * slim],
+            preferred_element_type=jnp.float32,
+        )
+
+    def take(side):
+        out_ref[:, side * slim : (side + 1) * slim] = gathered(side, free, blocks).astype(
+            out_ref.dtype
+        )
+
+    for side in range(1, sides - 1):
+        each(blocks, lambda block: late_sums(side, block).wait_recv(), free)
+        take(side)
+    each(detours, lambda index: home(index).wait_recv())
+    each(blocks, lambda block: late_sums(0, block).wait_recv(), direct(0))
+    take(0)
+    side = sides - 1
+    there = slice(side * slim, width)
+    each(blocks - 1, lambda block: late_sums(side, block).wait_recv(), free)
+    total[:, there] = gathered(side, free, blocks - 1)
+    late_sums(side, blocks - 1).wait_recv()
+    out_ref[:, there] = gathered(side, blocks - 1, blocks).astype(out_ref.dtype)
 
     told.wait_send()
     each(blocks, lambda block: dense(block).wait_send())
     each(free, lambda block: sums(block).wait_send())
-    for side in range(2):
-        each(blocks, lambda block: late_sums(side, block).wait_send(), free)
+    for side in range(sides):
+        each(blocks, lambda block: late_sums(side, block).wait_send(), direct(side))
+    each(detours, lambda index: out(index).wait_send())
+    each(detours, lambda index: home(index).wait_send())
 
     def sent(kind, index):
-        for stage in range(4):
+        straight = kind == 2 and index == sides - 1
+        for stage in (0, 4, 2, 3) if straight else range(4):
             weight_copy(stage, kind, index).wait_send()
 
     each(groups, lambda index: [sent(kind, index) for kind in range(2)])
-    for index in range(2 * pieces):
-        sent(2, index)
-
-
-def pair_scratch(tok_rows, width, hidden, fanout, capacity, blocks, groups, pieces):
+    for side in range(sides):
+        sent(2, side)
+
+
+def pair_scratch(tok_rows, width, hidden, fanout, capacity, blocks, groups, sides):
     dense = pltpu.VMEM((tok_rows, width), jnp.bfloat16)
     sums = pltpu.VMEM((tok_rows, width), jnp.float32)
     facts = pltpu.VMEM((8, tok_rows), jnp.float32)
@@ -655,8 +730,8 @@
     tall = pltpu.VMEM((hidden, width), jnp.bfloat16)
     by_block = pltpu.SemaphoreType.DMA((blocks,))
     by_group = pltpu.SemaphoreType.DMA((2, 4, groups))
-    by_piece = pltpu.SemaphoreType.DMA((4, 2 * pieces))
-    by_side = pltpu.SemaphoreType.DMA((2, blocks))
+    by_piece = pltpu.SemaphoreType.DMA((5, sides))
+    by_side = pltpu.SemaphoreType.DMA((sides, blocks))
     part = tok_rows // blocks
     late = tok_rows - (tok_rows - capacity) // part * part
     return [
@@ -664,9 +739,11 @@
         pltpu.VMEM((fanout, tok_rows), jnp.float32), pltpu.VMEM((2, width), jnp.float32),
         dense, dense, dense, wide, wide, tall, wide, wide, tall, dense, dense, sums, sums,
         facts, facts, facts, facts, pltpu.VMEM((7, tok_rows, LANES), jnp.float32),
-        pltpu.VMEM((late, hidden), jnp.bfloat16), dense, dense,
+        pltpu.VMEM((late, hidden), jnp.bfloat16), pltpu.VMEM((tok_rows, hidden), jnp.bfloat16),
+        pltpu.VMEM((late, width // sides), jnp.bfloat16), dense, dense,
         pltpu.SemaphoreType.DMA((8,)), pltpu.SemaphoreType.DMA((2,)),
         by_block, by_block, by_side, by_side, by_group, by_group, by_piece, by_piece,
+        by_block, by_block, by_block, by_block,
     ]
 
 
@@ -707,18 +784,19 @@
     near = pl.BlockSpec(memory_space=pltpu.VMEM)
     far = pl.BlockSpec(memory_space=pl.ANY)
     sems = pltpu.SemaphoreType.DMA((waves, devices))
-    blocks, groups, pieces = 8, 4, 2
+    blocks, groups, sides = 8, 4, 4
     paired = (
         devices == 4
-        and lax.axis_size("dp") % 4 == 0
+        and lax.axis_size("dp") % 8 == 0
         and tok_rows % (LANES * groups) == 0
         and tok_rows % (64 * blocks) == 0
         and width % (64 * groups) == 0
+        and width % (LANES * sides) == 0
         and hidden % 128 == 0
     )
     if paired:
-        kernel = functools.partial(pair_kernel, blocks, groups, pieces)
-        scratch = pair_scratch(tok_rows, width, hidden, fanout, capacity, blocks, groups, pieces)
+        kernel = functools.partial(pair_kernel, blocks, groups, sides)
+        scratch = pair_scratch(tok_rows, width, hidden, fanout, capacity, blocks, groups, sides)
     else:
         kernel = functools.partial(moe_kernel, devices)
         scratch = direct_scratch(tok_rows, width, hidden, buffer, sems)

time: 99.6 us -> 95.7 us (0.961)
  Pallas kernels: 98.1 us -> 94.2 us
    pallas_call x1, Pallas kernels: 98.1 us -> 94.2 us  [shards(): pl.pallas_call(kernel, out_shape=pltpu.VMEM((tok_rows, width), jnp.bfloat...]
where the time goes in v3:
time: 95.7 us; the launch traced here: 95.5 us
  Pallas kernels  94.2 us (98%)
  local copies, waits for them, and re-layouts  1.32 us (1%)
    pallas_call x1, Pallas kernels, shards(): pl.pallas_call(kernel, out_shape=pltpu.VMEM((tok_rows, width), jnp.bfloat...  94.2 us

profile of v3, /device:TPU:0, one launch (start us, length us, event | category | flops | bytes accessed | tf_op | source)
XLA Modules:
  0.0 95.5 jit_solution(14596000436619021204)
XLA Ops:
  0.0 94.2 %shard_map.82 = bf16[512,2048]{1,0:T(8,128)(2,1)S(1)} custom-call(bf16[512,2048]{1,0:T(8,128)(2,1)} %tokens_hbm.1, s32[1,512]{1,0:T(1,128)} %bitcast.5, s32[2,512]{1,0:T(2,128)} %bitcast.3, f32[2,512]{1,0:T(2,128)} %bitcast.4, f32[2,2048]{1,0:T(2,128)} %gain_hbm.1, bf16[2048,896]{1,0:T(8,128)(2,1)} %gate_hbm.1, bf16[2048,896]{1,0:T(8,128)(2,1)} %up_hbm.1, ...), custom_call_target="tpu_custom_call" | custom-call | tf_op jit(solution)/shard_map/pallas_call | solution.py:803
  94.2 1.3 %copy.10 = bf16[512,2048]{1,0:T(8,128)(2,1)} copy(bf16[512,2048]{1,0:T(8,128)(2,1)S(1)} %shard_map.82) | data formatting | bytes 4194304

commit v4 on v3

--- a/solution.py
+++ b/solution.py
@@ -272,14 +272,19 @@
     dense_recv,
     sum_send,
     sum_recv,
+    late_send,
+    late_recv,
     wide_send,
     wide_recv,
+    wide_join,
     tall_send,
     tall_recv,
+    tall_join,
     out_send,
     out_recv,
     home_send,
     home_recv,
+    entered,
 ):
     tok_rows, width = tokens.shape
     hidden = gate.shape[1]
@@ -299,6 +304,9 @@
     diagonal = (1 - me // 2) * 2 + 1 - me % 2
     other_layer = (layer // 2 * 2 + 1 - layer % 2) * 2 + core
     other_core = layer * 2 + 1 - core
+    beside_layers = 1 + (layer % 4 + 1) // 2 % 2
+    middle = beside_layers == 2
+    across_layer = (layer // 4 * 4 + 3 - layer % 4) * 2 + core
     far_layer = (layer // 4 * 4 + (layer + 2) % 4) * 2 + core
     quarter = layer % 2 * 2 + core
     layer_quarter = (1 - layer % 2) * 2 + core
@@ -316,67 +324,77 @@
     def part_rows(block):
         return pl.ds(pl.multiple_of(block * part, part), part)
 
-    def dense(block):
-        rows = part_rows(block)
+    share_of = blocks // groups
+    batch = tok_rows // groups
+
+    def batch_rows(group):
+        return pl.ds(pl.multiple_of(group * batch, batch), batch)
+
+    def dense_rows(rows, group):
         return remote(
             sorted_tokens.at[rows],
             near_tokens.at[rows],
-            dense_send.at[block],
-            dense_recv.at[block],
+            dense_send,
+            dense_recv.at[group],
             copy_of,
             first,
         )
 
+    def dense(block):
+        return dense_rows(part_rows(block), block // share_of)
+
+    def sums_rows(rows):
+        return remote(sum_out.at[rows], sum_in.at[rows], sum_send, sum_recv, copy_of, first)
+
     def sums(block):
-        rows = part_rows(block)
+        return sums_rows(part_rows(block))
+
+    slim = width // sides
+
+    def columns_of(side):
+        return pl.ds(side * slim, slim)
+
+    detours = blocks - free - 1
+
+    def late_rows(index):
+        begin = {0: free + detours, sides: blocks - 1}.get(index, free)
+        end = blocks - 1 if index == sides - 1 else blocks
+        return pl.ds(begin * part, (end - begin) * part)
+
+    def late_sums(index):
+        spot = (late_rows(index), columns_of(min(index, sides - 1)))
         return remote(
-            sum_out.at[rows],
-            sum_in.at[rows],
-            sum_send.at[0, block],
-            sum_recv.at[0, block],
+            sum_out.at[spot],
+            sum_in.at[spot],
+            late_send.at[index],
+            late_recv.at[index],
             copy_of,
             first,
         )
 
-    slim = width // sides
-
-    def columns_of(side):
-        return pl.ds(side * slim, slim)
-
-    def late_sums(side, block):
-        rows = part_rows(block)
+    def out_rows(begin, end, which):
+        rows = pl.ds(begin * part, (end - begin) * part)
         return remote(
-            sum_out.at[rows, columns_of(side)],
-            sum_in.at[rows, columns_of(side)],
-            sum_send.at[side, block],
-            sum_recv.at[side, block],
-            copy_of,
-            first,
-        )
-
-    detours = blocks - free - 1
-
-    def out(index):
-        rows = part_rows(index)
-        return remote(
-            sum_out.at[part_rows(free + index), columns_of(0)],
+            sum_out.at[pl.ds((free + begin) * part, (end - begin) * part), columns_of(0)],
             relayed.at[rows],
-            out_send.at[index],
-            out_recv.at[index],
+            out_send,
+            out_recv.at[which],
             far_layer,
             first,
         )
 
-    def home(index):
-        rows = part_rows(index)
+    def home_rows(begin, end):
         return remote(
-            relayed.at[rows],
-            sum_in.at[part_rows(free + index), columns_of(0)],
-            home_send.at[index],
-            home_recv.at[index],
+            relayed.at[pl.ds(begin * part, (end - begin) * part)],
+            sum_in.at[pl.ds((free + begin) * part, (end - begin) * part), columns_of(0)],
+            home_send,
+            home_recv,
             far_layer,
             me,
         )
+
+    cut = detours // 2
+    spans = ((0, cut), (cut, detours))
 
     wide_rows = width // 4 // groups
     tall_rows = hidden // 4
@@ -385,13 +403,20 @@
         which = layer_quarter if stage in (3, 4) else quarter
         if kind < 2:
             near, far = ((gate_hbm, far_gate), (up_hbm, far_up))[kind]
-            send, recv = wide_send.at[kind], wide_recv.at[kind]
+            send = wide_send.at[stage]
+            recv = wide_join if stage in (2, 3) else wide_recv.at[kind, stage, index]
             start = which * (width // 4) + index * wide_rows
             spot = (pl.ds(pl.multiple_of(start, wide_rows), wide_rows),)
         else:
-            near, far, send, recv = down_hbm, far_down, tall_send, tall_recv
+            near, far, send = down_hbm, far_down, tall_send.at[stage]
+            recv = tall_join.at[index] if stage in (2, 3) else tall_recv.at[stage % 3, index]
             start = which * tall_rows
             spot = (pl.ds(pl.multiple_of(start, tall_rows), tall_rows), columns_of(index))
+        return weight_remote(
+            stage, (near if stage in (0, 4) else far).at[spot], far.at[spot], send, recv
+        )
+
+    def weight_remote(stage, source, target, send, recv):
         copy, peer = (
             (copy_of, second),
             (other_layer, me),
@@ -399,14 +424,22 @@
             (other_core, me),
             (copy_of, second),
         )[stage]
-        return remote(
-            (near if stage in (0, 4) else far).at[spot],
-            far.at[spot],
-            send.at[stage, index],
-            recv.at[stage, index],
-            copy,
-            peer,
-        )
+        return remote(source, target, send, recv, copy, peer)
+
+    def wide_joined():
+        weight_remote(2, far_gate, far_gate, wide_send.at[2], wide_join).wait_recv()
+
+    def tall_joined(side):
+        both = far_down.at[pl.ds(0, 2 * tall_rows), columns_of(side)]
+        weight_remote(2, both, both, tall_send.at[2], tall_join.at[side]).wait_recv()
+
+    def weights_sent():
+        wide = far_gate.at[pl.ds(0, width // 2)]
+        for stage in range(4):
+            weight_remote(stage, wide, wide, wide_send.at[stage], wide_join).wait_send()
+        for stage, wholes in enumerate((sides, sides - 1, sides, sides, 1)):
+            tall = far_down.at[pl.ds(0, tall_rows), pl.ds(0, wholes * slim)]
+            weight_remote(stage, tall, tall, tall_send.at[stage], tall_join.at[0]).wait_send()
 
     def arrived_across(kind, index):
         weight_copy(0, kind, index).wait_recv()
@@ -442,21 +475,34 @@
     ]
     barrier = pltpu.get_barrier_semaphore()
     partners = (
-        (far_layer, first),
-        (far_layer, second),
-        (far_layer, me),
         (copy_of, first),
         (copy_of, second),
         (other_layer, me),
         (other_core, me),
     )
-    for copy, peer in partners:
+
+    def tell(semaphore, copy, peer):
         pl.semaphore_signal(
-            barrier,
+            semaphore,
             inc=1,
             device_id={"dp": copy, AXIS: peer},
             device_id_type=pl.DeviceIdType.MESH,
         )
+
+    def along_line(step):
+        step(other_layer)
+
+        @pl.when(middle)
+        def _():
+            step(across_layer)
+
+    for copy, peer in partners:
+        tell(barrier, copy, peer)
+
+    @pl.when(middle)
+    def _():
+        tell(barrier, across_layer, me)
+
     for load in loads[:5]:
         load.start()
     for load in loads[:3]:
@@ -500,8 +546,12 @@
     for load in loads[5:]:
         load.start()
     sort(0)
-    pl.semaphore_wait(barrier, len(partners))
+    sort(1)
+    pl.semaphore_wait(barrier, len(partners) - 1 + beside_layers)
+
     dense(0).start()
+    dense(1).start()
+    along_line(lambda copy: tell(entered.at[0], copy, me))
     each(groups, lambda index: [weight_copy(0, kind, index).start() for kind in range(2)])
     for side in range(sides):
         weight_copy(0, 2, side).start()
@@ -534,7 +584,7 @@
         sort(block)
         dense(block).start()
 
-    each(blocks, leave, 1)
+    each(blocks, leave, 2)
 
     def normalize(source, target, image, rows):
         values = source[rows, :].astype(jnp.float32)
@@ -562,13 +612,10 @@
         normalize(tokens, normed, columns[own_image, here, 0:1], here)
 
     each(tok_rows // rows, ready)
+    pl.semaphore_wait(entered.at[0], beside_layers)
+    along_line(lambda copy: tell(entered.at[1], copy, me))
     for load in loads[5:]:
         load.wait()
-
-    batch = tok_rows // groups
-
-    def batch_rows(group):
-        return pl.ds(pl.multiple_of(group * batch, batch), batch)
 
     double = 2 * batch
 
@@ -602,17 +649,16 @@
         def _():
             arrived_across(2, 0)
 
-        for index in range(blocks // groups):
-            dense(group * (blocks // groups) + index).wait_recv()
         here = batch_rows(group)
+        dense_rows(here, group).wait_recv()
         for start in range(0, batch, rows):
             few = pl.ds(pl.multiple_of(group * batch + start, rows), rows)
             normalize(near_tokens, near_normed, columns[near_image, few, 0:1], few)
         near = columns[near_mine, here, 0:1] * feed(near_normed[here, :], gate, up, down)
         near_total[here, :] = near
         sum_out[here, :] = near.astype(jnp.bfloat16)
-        for index in range(blocks // groups):
-            block = group * (blocks // groups) + index
+        for index in range(share_of):
+            block = group * share_of + index
 
             @pl.when(block < free)
             def _():
@@ -624,31 +670,28 @@
     arrived_along(1, groups - 1)
     arrived_across(2, 1)
 
-    def joined(kind, index):
-        weight_copy(2, kind, index).wait_recv()
-        weight_copy(3, kind, index).wait_recv()
-
     late = slice(free * part, tok_rows)
-    each(groups, lambda index: [joined(kind, index) for kind in range(2)])
+    wide_joined()
     active[...] = activate(near_normed[late, :], far_gate, far_up)
 
     def finish(side):
-        joined(2, side)
+        tall_joined(side)
         there = slice(side * slim, (side + 1) * slim)
         sum_out[late, there] = (
             near_total[late, there]
             + columns[near_far, late, 0:1] * settle(active[...], far_down[:, there])
         ).astype(jnp.bfloat16)
         if side == 0:
-            each(detours, lambda index: out(index).start())
-        each(blocks, lambda block: late_sums(side, block).start(), direct(side))
-
-    def direct(side):
-        return free + detours if side == 0 else free
-
-    def pass_on(index):
-        out(index).wait_recv()
-        home(index).start()
+            for which, (begin, end) in enumerate(spans):
+                out_rows(begin, end, which).start()
+        late_sums(side).start()
+        if side == sides - 1:
+            late_sums(sides).start()
+
+    def pass_on(which):
+        begin, end = spans[which]
+        out_rows(begin, end, which).wait_recv()
+        home_rows(begin, end).start()
 
     def own(group):
         here = pair_rows(group)
@@ -658,6 +701,7 @@
         there = slice(side * slim, (side + 1) * slim)
         total[:, there] += columns[own_far, :, 0:1] * settle(own_active[...], far_down[:, there])
 
+    pl.semaphore_wait(entered.at[1], beside_layers)
     arrived_along(2, 0)
     finish(0)
     arrived_across(2, 2)
@@ -667,12 +711,12 @@
     arrived_across(2, 3)
     arrived_along(2, 2)
     finish(2)
-    each(detours // 2, pass_on)
+    pass_on(0)
     each(tok_rows // double, own, 1)
     arrived_along(2, 3)
     finish(3)
-    each(detours, pass_on, detours // 2)
-    each(free, lambda block: sums(block).wait_recv())
+    pass_on(1)
+    sums_rows(pl.ds(0, free * part)).wait_recv()
     total[...] += jnp.dot(
         places(0, free * part), sum_in[: free * part, :], preferred_element_type=jnp.float32
     )
@@ -692,34 +736,28 @@
         )
 
     for side in range(1, sides - 1):
-        each(blocks, lambda block: late_sums(side, block).wait_recv(), free)
+        late_sums(side).wait_recv()
         take(side)
-    each(detours, lambda index: home(index).wait_recv())
-    each(blocks, lambda block: late_sums(0, block).wait_recv(), direct(0))
+    home_rows(0, detours).wait_recv()
+    late_sums(0).wait_recv()
     take(0)
+    told.wait_send()
+    dense_rows(pl.ds(0, tok_rows), 0).wait_send()
+    sums_rows(pl.ds(0, free * part)).wait_send()
+    for side in range(sides - 1):
+        late_sums(side).wait_send()
+    out_rows(0, detours, 0).wait_send()
+    home_rows(0, detours).wait_send()
+    weights_sent()
+
     side = sides - 1
     there = slice(side * slim, width)
-    each(blocks - 1, lambda block: late_sums(side, block).wait_recv(), free)
+    late_sums(side).wait_recv()
     total[:, there] = gathered(side, free, blocks - 1)
-    late_sums(side, blocks - 1).wait_recv()
+    late_sums(sides).wait_recv()
     out_ref[:, there] = gathered(side, blocks - 1, blocks).astype(out_ref.dtype)
-
-    told.wait_send()
-    each(blocks, lambda block: dense(block).wait_send())
-    each(free, lambda block: sums(block).wait_send())
-    for side in range(sides):
-        each(blocks, lambda block: late_sums(side, block).wait_send(), direct(side))
-    each(detours, lambda index: out(index).wait_send())
-    each(detours, lambda index: home(index).wait_send())
-
-    def sent(kind, index):
-        straight = kind == 2 and index == sides - 1
-        for stage in (0, 4, 2, 3) if straight else range(4):
-            weight_copy(stage, kind, index).wait_send()
-
-    each(groups, lambda index: [sent(kind, index) for kind in range(2)])
-    for side in range(sides):
-        sent(2, side)
+    late_sums(side).wait_send()
+    late_sums(sides).wait_send()
 
 
 def pair_scratch(tok_rows, width, hidden, fanout, capacity, blocks, groups, sides):
@@ -728,10 +766,8 @@
     facts = pltpu.VMEM((8, tok_rows), jnp.float32)
     wide = pltpu.VMEM((width, hidden), jnp.bfloat16)
     tall = pltpu.VMEM((hidden, width), jnp.bfloat16)
-    by_block = pltpu.SemaphoreType.DMA((blocks,))
-    by_group = pltpu.SemaphoreType.DMA((2, 4, groups))
-    by_piece = pltpu.SemaphoreType.DMA((5, sides))
-    by_side = pltpu.SemaphoreType.DMA((sides, blocks))
+    semaphores = pltpu.SemaphoreType.DMA
+    one = semaphores(())
     part = tok_rows // blocks
     late = tok_rows - (tok_rows - capacity) // part * part
     return [
@@ -741,9 +777,11 @@
         facts, facts, facts, facts, pltpu.VMEM((7, tok_rows, LANES), jnp.float32),
         pltpu.VMEM((late, hidden), jnp.bfloat16), pltpu.VMEM((tok_rows, hidden), jnp.bfloat16),
         pltpu.VMEM((late, width // sides), jnp.bfloat16), dense, dense,
-        pltpu.SemaphoreType.DMA((8,)), pltpu.SemaphoreType.DMA((2,)),
-        by_block, by_block, by_side, by_side, by_group, by_group, by_piece, by_piece,
-        by_block, by_block, by_block, by_block,
+        semaphores((8,)), semaphores((2,)), one, semaphores((groups,)), one, one,
+        semaphores((sides + 1,)), semaphores((sides + 1,)),
+        semaphores((4,)), semaphores((2, 2, groups)), one,
+        semaphores((5,)), semaphores((2, sides)), semaphores((sides,)),
+        one, semaphores((2,)), one, one, pltpu.SemaphoreType.REGULAR((2,)),
     ]
 
 

time: 95.7 us -> 93.3 us (0.975)
  Pallas kernels: 94.2 us -> 91.7 us
    pallas_call x1, Pallas kernels: 94.2 us -> 91.7 us  [shards(): pl.pallas_call(kernel, out_shape=pltpu.VMEM((tok_rows, width), jnp.bfloat...]
where the time goes in v4:
time: 93.3 us; the launch traced here: 93.1 us
  Pallas kernels  91.7 us (98%)
  local copies, waits for them, and re-layouts  1.32 us (1%)
    pallas_call x1, Pallas kernels, shards(): pl.pallas_call(kernel, out_shape=pltpu.VMEM((tok_rows, width), jnp.bfloat...  91.7 us

profile of v4, /device:TPU:0, one launch (start us, length us, event | category | flops | bytes accessed | tf_op | source)
XLA Modules:
  0.0 93.1 jit_solution(17529224150008017299)
XLA Ops:
  0.0 91.7 %shard_map.82 = bf16[512,2048]{1,0:T(8,128)(2,1)S(1)} custom-call(bf16[512,2048]{1,0:T(8,128)(2,1)} %tokens_hbm.1, s32[1,512]{1,0:T(1,128)} %bitcast.5, s32[2,512]{1,0:T(2,128)} %bitcast.3, f32[2,512]{1,0:T(2,128)} %bitcast.4, f32[2,2048]{1,0:T(2,128)} %gain_hbm.1, bf16[2048,896]{1,0:T(8,128)(2,1)} %gate_hbm.1, bf16[2048,896]{1,0:T(8,128)(2,1)} %up_hbm.1, ...), custom_call_target="tpu_custom_call" | custom-call | tf_op jit(solution)/shard_map/pallas_call | solution.py:841
  91.8 1.3 %copy.10 = bf16[512,2048]{1,0:T(8,128)(2,1)} copy(bf16[512,2048]{1,0:T(8,128)(2,1)S(1)} %shard_map.82) | data formatting | bytes 4194304

commit v5 on v4

--- a/solution.py
+++ b/solution.py
@@ -260,6 +260,7 @@
     sorted_facts,
     near_facts,
     slots,
+    earlier,
     columns,
     active,
     own_active,
@@ -394,7 +395,7 @@
         )
 
     cut = detours // 2
-    spans = ((0, cut), (cut, detours))
+    spans = tuple((begin, begin + 1) for begin in range(detours))
 
     wide_rows = width // 4 // groups
     tall_rows = hidden // 4
@@ -505,34 +506,25 @@
 
     for load in loads[:5]:
         load.start()
-    for load in loads[:3]:
-        load.wait()
-
+    earlier[...] = jnp.where(
+        lax.broadcasted_iota(jnp.int32, (tok_rows, tok_rows), 0)
+        < lax.broadcasted_iota(jnp.int32, (tok_rows, tok_rows), 1),
+        1.0,
+        0.0,
+    ).astype(jnp.bfloat16)
     lines = 8
     expert = lax.broadcasted_iota(jnp.int32, (lines, tok_rows), 0)
-    named = jnp.zeros((lines, tok_rows), jnp.float32)
-    share = jnp.where(
-        expert == devices,
-        jnp.broadcast_to(modality_ref[...].astype(jnp.float32), (lines, tok_rows)),
-        0.0,
-    )
-    late = jnp.zeros((1, tok_rows), jnp.float32)
+    loads[0].wait()
+    late_ones = jnp.zeros((1, tok_rows), jnp.float32)
     for k in range(fanout):
-        share = jnp.where(expert == ids_ref[k : k + 1, :], weights_ref[k : k + 1, :], share)
-        late = jnp.where(ids_ref[k : k + 1, :] == diagonal, 1.0, late)
-    facts[...] = share
-    named = jnp.where(expert == 0, late, 1.0 - late)
-    before = (
-        lax.broadcasted_iota(jnp.int32, (tok_rows, tok_rows), 0)
-        < lax.broadcasted_iota(jnp.int32, (tok_rows, tok_rows), 1)
-    )
+        late_ones = jnp.where(ids_ref[k : k + 1, :] == diagonal, 1.0, late_ones)
+    named = jnp.where(expert == 0, late_ones, 1.0 - late_ones)
     count = jnp.dot(
-        named.astype(jnp.bfloat16),
-        jnp.where(before, 1.0, 0.0).astype(jnp.bfloat16),
-        preferred_element_type=jnp.float32,
+        named.astype(jnp.bfloat16), earlier[...], preferred_element_type=jnp.float32
     )
     slots[...] = jnp.broadcast_to(
-        jnp.where(late > 0.5, tok_rows - 1.0 - count[0:1, :], count[1:2, :]), (lines, tok_rows)
+        jnp.where(late_ones > 0.5, tok_rows - 1.0 - count[0:1, :], count[1:2, :]),
+        (lines, tok_rows),
     )
 
     def sort(block):
@@ -543,19 +535,30 @@
         ).astype(jnp.bfloat16)
 
     loads[3].wait()
-    for load in loads[5:]:
-        load.start()
     sort(0)
+    pl.semaphore_wait(barrier, len(partners) - 1 + beside_layers)
+
+    dense(0).start()
     sort(1)
-    pl.semaphore_wait(barrier, len(partners) - 1 + beside_layers)
-
-    dense(0).start()
     dense(1).start()
     along_line(lambda copy: tell(entered.at[0], copy, me))
     each(groups, lambda index: [weight_copy(0, kind, index).start() for kind in range(2)])
     for side in range(sides):
         weight_copy(0, 2, side).start()
     weight_copy(4, 2, sides - 1).start()
+
+    for load in loads[5:]:
+        load.start()
+    for load in loads[1:3]:
+        load.wait()
+    share = jnp.where(
+        expert == devices,
+        jnp.broadcast_to(modality_ref[...].astype(jnp.float32), (lines, tok_rows)),
+        0.0,
+    )
+    for k in range(fanout):
+        share = jnp.where(expert == ids_ref[k : k + 1, :], weights_ref[k : k + 1, :], share)
+    facts[...] = share
 
     def keep(place, line):
         columns[place] = jnp.broadcast_to(line, (LANES, tok_rows)).T
@@ -711,11 +714,13 @@
     arrived_across(2, 3)
     arrived_along(2, 2)
     finish(2)
-    pass_on(0)
+    for which in range(cut):
+        pass_on(which)
     each(tok_rows // double, own, 1)
     arrived_along(2, 3)
     finish(3)
-    pass_on(1)
+    for which in range(cut, detours):
+        pass_on(which)
     sums_rows(pl.ds(0, free * part)).wait_recv()
     total[...] += jnp.dot(
         places(0, free * part), sum_in[: free * part, :], preferred_element_type=jnp.float32
@@ -774,14 +779,15 @@
         pltpu.VMEM((1, tok_rows), jnp.int32), pltpu.VMEM((fanout, tok_rows), jnp.int32),
         pltpu.VMEM((fanout, tok_rows), jnp.float32), pltpu.VMEM((2, width), jnp.float32),
         dense, dense, dense, wide, wide, tall, wide, wide, tall, dense, dense, sums, sums,
-        facts, facts, facts, facts, pltpu.VMEM((7, tok_rows, LANES), jnp.float32),
+        facts, facts, facts, facts, pltpu.VMEM((tok_rows, tok_rows), jnp.bfloat16),
+        pltpu.VMEM((7, tok_rows, LANES), jnp.float32),
         pltpu.VMEM((late, hidden), jnp.bfloat16), pltpu.VMEM((tok_rows, hidden), jnp.bfloat16),
         pltpu.VMEM((late, width // sides), jnp.bfloat16), dense, dense,
         semaphores((8,)), semaphores((2,)), one, semaphores((groups,)), one, one,
         semaphores((sides + 1,)), semaphores((sides + 1,)),
         semaphores((4,)), semaphores((2, 2, groups)), one,
         semaphores((5,)), semaphores((2, sides)), semaphores((sides,)),
-        one, semaphores((2,)), one, one, pltpu.SemaphoreType.REGULAR((2,)),
+        one, semaphores((late // part - 1,)), one, one, pltpu.SemaphoreType.REGULAR((2,)),
     ]
 
 
@@ -825,6 +831,7 @@
     blocks, groups, sides = 8, 4, 4
     paired = (
         devices == 4
+        and fanout == 2
         and lax.axis_size("dp") % 8 == 0
         and tok_rows % (LANES * groups) == 0
         and tok_rows % (64 * blocks) == 0

time: 93.3 us -> 92.9 us (level)
  no operation moved by 1% of the time
where the time goes in v5:
time: 92.9 us; the launch traced here: 92.7 us
  Pallas kernels  91.4 us (98%)
  local copies, waits for them, and re-layouts  1.32 us (1%)
    pallas_call x1, Pallas kernels, shards(): pl.pallas_call(kernel, out_shape=pltpu.VMEM((tok_rows, width), jnp.bfloat...  91.4 us

profile of v5, /device:TPU:0, one launch (start us, length us, event | category | flops | bytes accessed | tf_op | source)
XLA Modules:
  0.0 92.7 jit_solution(9931154361673377425)
XLA Ops:
  0.0 91.4 %shard_map.82 = bf16[512,2048]{1,0:T(8,128)(2,1)S(1)} custom-call(bf16[512,2048]{1,0:T(8,128)(2,1)} %tokens_hbm.1, s32[1,512]{1,0:T(1,128)} %bitcast.5, s32[2,512]{1,0:T(2,128)} %bitcast.3, f32[2,512]{1,0:T(2,128)} %bitcast.4, f32[2,2048]{1,0:T(2,128)} %gain_hbm.1, bf16[2048,896]{1,0:T(8,128)(2,1)} %gate_hbm.1, bf16[2048,896]{1,0:T(8,128)(2,1)} %up_hbm.1, ...), custom_call_target="tpu_custom_call" | custom-call | tf_op jit(solution)/shard_map/pallas_call | solution.py:848
  91.4 1.3 %copy.10 = bf16[512,2048]{1,0:T(8,128)(2,1)} copy(bf16[512,2048]{1,0:T(8,128)(2,1)S(1)} %shard_map.82) | data formatting | bytes 4194304
